TPU v7x, 256 devices: a 4x2x16 block of a 4x16x16 slice. The times are simulated.
256 devices in a mesh: group: 2 (over y), temp: 4 (over x), gz: 32 (over z, core).
Axes of the slice: x: 4, y: 2, z: 16, core: 2. Of those that a mesh axis runs over, the one named last changes fastest.
The devices are a block of a 4x16x16 slice.
Arguments:
- spin_state: float32 [16, 3, 128, 128, 128], P(('group', 'temp'), None, 'gz'), parts along dimension 0, may hold values from -1 to 1, as said below
- couplings: float32 [3, 256, 128, 128], P(None, ('group', 'gz')), parts along dimension 1, may hold values from -12 to 12
- inverse_temps: float32 [16], P(('group', 'temp')), parts along dimension 0, may hold values from 0.3 to 3
- colour_order: int32 [16], P(('group', 'temp')), parts along dimension 0, may hold values 0 or 1
- heat_level: float32 [16, 128, 128, 128], P(('group', 'temp'), 'gz'), parts along dimension 0, may hold values from 0.001 to 0.999
- heat_height: float32 [16, 128, 128, 128], P(('group', 'temp'), 'gz'), parts along dimension 0, may hold values from -1 to 1
- heat_angle: float32 [16, 128, 128, 128], P(('group', 'temp'), 'gz'), parts along dimension 0, may hold values from -3.140625 to 3.140625
- swap_bits: int32 [16], P(('group', 'temp')), parts along dimension 0, may hold values 0 or 1
Outputs:
- spin_final: float32 [16, 3, 128, 128, 128], P(('group', 'temp'), None, 'gz'), parts along dimension 0
- energies: float32 [16], P(('group', 'temp')), parts along dimension 0
There are 2 independent parts, one for each index of `group`. A program takes and returns all parts, laid end to end along the dimension named above; each array names one. Nothing has to cross between parts.
Inputs may be any that keep to these rules, and one draw needn't show every extreme that they name: `spin_state`: every site's three components form a vector of unit length.
All inputs are finite; a program needn't handle non-finite values. No bound on the sum of `colour_order` or of `swap_bits` on one device may be relied on, other than what follows from the above.
Results may differ from a plain program's by a relative error of at most 0.0003.
Values sent between devices are 32-bit elements; how exact they have to be, the bound alone decides.
A program may use at most 64 MiB of HBM per device.

v0:
```python
import jax
import jax.numpy as jnp
from jax import lax
from jax.sharding import PartitionSpec as P

OR_SWEEPS = 2


def passed_along(value, axis, steps):
    count = lax.axis_size(axis)
    pairs = [(source, (source + steps) % count) for source in range(count)]
    return lax.ppermute(value, axis, pairs)


def extended(array, sides, width):
    for axis, dim in sides:
        count, length = (lax.axis_size(axis), array.shape[dim])
        up = [(i, (i + 1) % count) for i in range(count)]
        down = [(j, i) for i, j in up]
        last = lax.slice_in_dim(array, length - width, length, axis=dim)
        leading = lax.slice_in_dim(array, 0, width, axis=dim)
        before = lax.ppermute(last, axis, up)
        after = lax.ppermute(leading, axis, down)
        array = jnp.concatenate([before, array, after], axis=dim)
    return array


def copy_for_each(array, axis):
    copies = jnp.broadcast_to(array, (lax.axis_size(axis), *array.shape))
    return lax.all_to_all(copies, axis, split_axis=0, concat_axis=0, tiled=True)


def of_everyone(array, axis):
    everything = copy_for_each(array, axis)
    return jnp.sum(everything, axis=0)


def shifted(block, axis, distance):
    devices = range(lax.axis_size(axis))
    route = [(i - distance, i) for i in devices if i - distance in devices]
    return lax.ppermute(block, axis, route)


def reflect(current, pulled):
    projection = jnp.sum(current * pulled, axis=1, keepdims=True)
    square = jnp.sum(pulled * pulled, axis=1, keepdims=True)
    return 2.0 * projection / jnp.maximum(square, 0.01) * pulled - current


def heat_bath(pulled, beta_value, uniform_level, cosine_draw, angle_draw):
    square = jnp.sum(pulled * pulled, axis=1, keepdims=True)
    strength = jnp.sqrt(jnp.maximum(square, 0.01))
    unit_axis = pulled / strength
    reach = beta_value * strength
    cosine = 1.0 + jnp.log1p(uniform_level * jnp.expm1(-2.0 * reach)) / reach
    side = jnp.sqrt(jnp.maximum(1.0 - cosine_draw * cosine_draw, 0.0))
    proposal = jnp.concatenate(
        [side * jnp.cos(angle_draw), side * jnp.sin(angle_draw), cosine_draw], axis=1
    )
    along_axis = jnp.sum(proposal * unit_axis, axis=1, keepdims=True)
    tangent = proposal - along_axis * unit_axis
    tangent = tangent / jnp.sqrt(
        jnp.maximum(jnp.sum(tangent * tangent, axis=1, keepdims=True), 0.0001)
    )
    return cosine * unit_axis + jnp.sqrt(jnp.maximum(1.0 - cosine * cosine, 0.0)) * tangent


def local_pull(padded, bond_pad, first_plane, end_plane):
    middle = padded[:, :, first_plane:end_plane]
    east_bond = bond_pad[0, first_plane:end_plane]
    north_bond = bond_pad[1, first_plane:end_plane]
    pulled = east_bond * jnp.roll(middle, -1, 4) + jnp.roll(east_bond, 1, 2) * jnp.roll(
        middle, 1, 4
    )
    pulled = (
        pulled
        + north_bond * jnp.roll(middle, -1, 3)
        + jnp.roll(north_bond, 1, 1) * jnp.roll(middle, 1, 3)
    )
    pulled = (
        pulled + bond_pad[2, first_plane:end_plane] * padded[:, :, first_plane + 1 : end_plane + 1]
    )
    pulled = (
        pulled
        + bond_pad[2, first_plane - 1 : end_plane - 1]
        * padded[:, :, first_plane - 1 : end_plane - 1]
    )
    return (middle, pulled)


def colour_mask(colour_order, plane_start, count, row_count, column_count, colour):
    plane_index = plane_start + jnp.arange(count, dtype=jnp.int32)
    row_index = jnp.arange(row_count, dtype=jnp.int32)
    column_index = jnp.arange(column_count, dtype=jnp.int32)
    site_sum = plane_index[:, None, None] + row_index[None, :, None] + column_index[None, None, :]
    parity = (site_sum[None] + colour_order[:, None, None, None]) % 2
    return (parity == colour)[:, None]


def relax_planes(padded, bond_pad, first_plane, end_plane, chosen):
    middle, pulled = local_pull(padded, bond_pad, first_plane, end_plane)
    renewed = jnp.where(chosen, reflect(middle, pulled), middle)
    return jnp.concatenate([padded[:, :, :first_plane], renewed, padded[:, :, end_plane:]], axis=2)


def pair_swap(stacked, decisions):
    flipped = stacked[:, ::-1]
    taking = (decisions != 0).reshape((-1,) + (1,) * (stacked.ndim - 1))
    return jnp.where(taking, flipped, stacked)


def on_device(
    spin_state,
    couplings,
    inverse_temps,
    colour_order,
    heat_level,
    heat_height,
    heat_angle,
    swap_bits,
):
    replica_count, _, planes, row_count, column_count = spin_state.shape
    plane_offset = lax.axis_index("gz") * planes
    spin_now = spin_state
    lower_upward = passed_along(couplings[2:3, -1:], "gz", 1)
    lower_plane = jnp.concatenate(
        [jnp.zeros((2, 1, row_count, column_count), jnp.float32), lower_upward], axis=0
    )
    bond_near = jnp.concatenate([lower_plane, couplings], axis=1)
    for sweep_index in range(OR_SWEEPS):
        for colour in (0, 1):
            chosen = colour_mask(
                colour_order, plane_offset, planes, row_count, column_count, colour
            )
            padded = extended(spin_now, (("gz", 2),), 1)
            padded = relax_planes(padded, bond_near, 1, planes + 1, chosen)
            spin_now = padded[:, :, 1:-1]
    beta_value = inverse_temps[:, None, None, None, None]
    last_pull = None
    last_chosen = None
    for colour in (0, 1):
        chosen = colour_mask(colour_order, plane_offset, planes, row_count, column_count, colour)
        padded = extended(spin_now, (("gz", 2),), 1)
        middle, pulled = local_pull(padded, bond_near, 1, planes + 1)
        renewed = heat_bath(
            pulled, beta_value, heat_level[:, None], heat_height[:, None], heat_angle[:, None]
        )
        spin_now = jnp.where(chosen, renewed, middle)
        last_pull = pulled
        last_chosen = chosen
    site_terms = jnp.sum(spin_now * last_pull, axis=1, keepdims=True)
    local_energy = -jnp.sum(jnp.where(last_chosen, site_terms, 0.0), axis=(1, 2, 3, 4))
    total_sites = float(column_count * row_count * planes * lax.axis_size("gz"))
    energy_now = of_everyone(local_energy, "gz") / total_sites
    tail_shape = spin_now.shape[1:]
    pair_count = replica_count // 2
    spin_now = pair_swap(spin_now.reshape((pair_count, 2) + tail_shape), swap_bits[0::2]).reshape(
        spin_now.shape
    )
    energy_now = pair_swap(energy_now.reshape((pair_count, 2)), swap_bits[0::2]).reshape(
        (replica_count,)
    )
    top_send = (spin_now[-1:], energy_now[-1:], swap_bits[-1:].astype(jnp.float32))
    below_spin, below_energy, below_bit = shifted(
        (top_send[0], top_send[1], top_send[2]), "temp", 1
    )
    above_spin, above_energy = shifted((spin_now[:1], energy_now[:1]), "temp", -1)
    top_device = lax.axis_index("temp") == lax.axis_size("temp") - 1
    odd_bits = swap_bits[1::2]
    odd_bits = jnp.where((jnp.arange(pair_count) == pair_count - 1) & top_device, 0, odd_bits)
    pair_bits = jnp.concatenate([(below_bit > 0.5).astype(jnp.int32), odd_bits])
    widened = jnp.concatenate([below_spin, spin_now, above_spin], axis=0)
    widened = pair_swap(widened.reshape((pair_count + 1, 2) + tail_shape), pair_bits)
    spin_final = widened.reshape((replica_count + 2,) + tail_shape)[1:-1]
    energy_wide = jnp.concatenate([below_energy, energy_now, above_energy], axis=0)
    energy_wide = pair_swap(energy_wide.reshape((pair_count + 1, 2)), pair_bits)
    energies = energy_wide.reshape((replica_count + 2,))[1:-1]
    return (spin_final, energies)


def solution(mesh):
    return jax.shard_map(
        on_device,
        mesh=mesh,
        in_specs=(
            P(("group", "temp"), None, "gz", None, None),
            P(None, ("group", "gz"), None, None),
            P(("group", "temp")),
            P(("group", "temp")),
            P(("group", "temp"), "gz", None, None),
            P(("group", "temp"), "gz", None, None),
            P(("group", "temp"), "gz", None, None),
            P(("group", "temp")),
        ),
        out_specs=(P(("group", "temp"), None, "gz", None, None), P(("group", "temp"))),
        check_vma=False,
    )
```

profile of v0, /device:TPU:40, one launch (start us, length us, event | category | flops | bytes accessed | tf_op | source)
XLA Modules:
  0.0 159.3 jit_solution(2242881543556269519)
XLA Ops:
  0.7 1.6 slice.366
  2.2 1.9 %fusion.81 = (f32[2,3,1,128,128]{4,3,2,1,0:T(8,128)}, f32[2,3,1,128,128]{4,3,2,1,0:T(8,128)S(1)}) fusion(f32[2,3,4,128,128]{4,3,2,1,0:T(8,128)} %param.8), kind=kLoop, calls=%fused_computation.178 | loop fusion | bytes 1572864 | tf_op jit(solution)/shard_map/slice | solution.py:21
  4.2 21.9 %collective-permute-start.1 = (f32[2,3,1,128,128]{4,3,2,1,0:T(8,128)}, f32[2,3,1,128,128]{4,3,2,1,0:T(8,128)}, u32[]{:S(2)}, u32[]{:S(2)}) collective-permute-start(f32[2,3,1,128,128]{4,3,2,1,0:T(8,128)} %get-tuple-element.84), channel_id=1, source_target_pairs={{1,0},{2,1},{3,2},{4,3},{5,4},{6,5},{7,6},{8,7},{9,8},{10,9},{11,1... | collective-permute-start | bytes 1179656 | tf_op jit(solution)/shard_map/ppermute | solution.py:23
  26.1 0.6 fusion.83
  27.3 4.8 %collective-permute-start = (f32[1]{0:T(128)}, f32[1]{0:T(128)}, u32[]{:S(2)}, u32[]{:S(2)}) collective-permute-start(f32[1]{0:T(128)} %convert_element_type.6), channel_id=1, source_target_pairs={{0,32},{32,64},{64,96},{1,33},{33,65},{65,97},{2,34},{34,66},{66,9... | collective-permute-start | bytes 20 | tf_op jit(solution)/shard_map/ppermute | solution.py:41
  32.2 2.2 %fusion.77 = (f32[2,3,4,128,127]{4,3,2,1,0:T(8,128)}, f32[2,3,4,128,127]{4,3,2,1,0:T(8,128)}) fusion(f32[2,3,4,128,128]{4,3,2,1,0:T(8,128)S(1)} %copy-done), kind=kLoop, calls=%fused_computation.174 | loop fusion | bytes 6242304 | tf_op jit(solution)/shard_map/jit(_roll_static)/slice | solution.py:72
  34.4 2.2 %fusion.78 = (f32[2,3,4,128,1]{4,3,2,1,0:T(8,128)}, f32[2,3,4,128,1]{4,3,2,1,0:T(8,128)}) fusion(f32[2,3,4,128,128]{4,3,2,1,0:T(8,128)S(1)} %copy-done), kind=kLoop, calls=%fused_computation.175 | loop fusion | bytes 49152 | tf_op jit(solution)/shard_map/jit(_roll_static)/slice | solution.py:72
  36.6 1.9 %fusion.79 = (f32[2,3,4,127,128]{4,3,2,1,0:T(8,128)}, f32[2,3,4,127,128]{4,3,2,1,0:T(8,128)}) fusion(f32[2,3,4,128,128]{4,3,2,1,0:T(8,128)S(1)} %copy-done), kind=kLoop, calls=%fused_computation.176 | loop fusion | bytes 6242304 | tf_op jit(solution)/shard_map/jit(_roll_static)/slice | solution.py:77
  38.6 0.6 fusion.80
  41.2 3.7 %multiply_bitcast_fusion.1 = (f32[2,1,4,128,128]{4,3,2,1,0:T(8,128)S(1)}, f32[2,1,4,128,128]{4,3,2,1,0:T(8,128)S(1)}) fusion(f32[2,4,128,128]{3,2,1,0:T(8,128)} %param.14, f32[2,4,128,128]{3,2,1,0:T(8,128)S(1)} %copy-done.1), kind=kLoop, calls=%fused_computation.122 | loop fusion | flops 655360 | bytes 2097152 | tf_op jit(solution)/shard_map/mul | solution.py:58
  45.7 1.1 slice_bitcast_fusion.4
  47.1 1.1 copy-done.2
  48.2 3.9 %multiply_reduce_fusion.14 = (f32[2,4,128,128]{3,2,1,0:T(8,128)S(1)}, f32[2,4,128,128]{3,2,1,0:T(8,128)S(1)}, f32[2,3,4,128,128]{4,3,2,1,0:T(8,128)S(1)}) fusion(f32[2,3,4,128,128]{4,3,2,1,0:T(8,128)S(1)} %copy-done, f32[2,3,1,128,128]{4,3,2,1,0:T(8,128)} %collective-permute-done.3, f32[4,128,128]{2,1,0:T(8,128)S(1)} %get-tuple-element.91, ...), kind=kLoop, calls=%fused_computation.104 | loop fusion | flops 7995392 | bytes 12845056 | tf_op jit(solution)/shard_map/reduce_sum | solution.py:45
  53.7 2.1 %collective-permute-start.4 = (f32[2,3,1,128,128]{4,3,2,1,0:T(8,128)S(1)}, f32[2,3,1,128,128]{4,3,2,1,0:T(8,128)S(1)}, u32[]{:S(2)}, u32[]{:S(2)}) collective-permute-start(f32[2,3,1,128,128]{4,3,2,1,0:T(8,128)S(1)} %get-tuple-element.74), channel_id=1, source_target_pairs={{1,0},{2,1},{3,2},{4,3},{5,4},{6,5},{7,6},{8,7},{9,8},{10,9},{11,1... | collective-permute-start | bytes 1179656 | tf_op jit(solution)/shard_map/ppermute | solution.py:23
  56.2 4.9 %collective-permute-done.4 = f32[2,3,1,128,128]{4,3,2,1,0:T(8,128)S(1)} collective-permute-done((f32[2,3,1,128,128]{4,3,2,1,0:T(8,128)S(1)}, f32[2,3,1,128,128]{4,3,2,1,0:T(8,128)S(1)}, u32[]{:S(2)}, u32[]{:S(2)}) %collective-permute-start.4) | collective-permute-done | bytes 393248 | tf_op jit(solution)/shard_map/ppermute | solution.py:23
  61.1 3.1 %collective-permute-done.5 = f32[2,3,1,128,128]{4,3,2,1,0:T(8,128)S(1)} collective-permute-done((f32[2,3,1,128,128]{4,3,2,1,0:T(8,128)S(1)}, f32[2,3,1,128,128]{4,3,2,1,0:T(8,128)S(1)}, u32[]{:S(2)}, u32[]{:S(2)}) %collective-permute-start.5) | collective-permute-done | bytes 393248 | tf_op jit(solution)/shard_map/ppermute | solution.py:22
  64.3 2.3 %multiply_reduce_fusion.12 = (f32[2,4,128,128]{3,2,1,0:T(8,128)S(1)}, f32[2,4,128,128]{3,2,1,0:T(8,128)S(1)}, f32[2,3,4,128,128]{4,3,2,1,0:T(8,128)S(1)}) fusion(f32[2,3,4,128,128]{4,3,2,1,0:T(8,128)S(1)} %subtract_select_fusion.3, f32[2,3,1,128,128]{4,3,2,1,0:T(8,128)S(1)} %collective-permute-done.5, f32[4,128,128]{2,1,0:T(8,128)S(1)} %get-tuple-element.91, ...), kind=kLoop, calls=%fused_computation.102 | loop fusion | flops 7995392 | bytes 12845056 | tf_op jit(solution)/shard_map/reduce_sum | solution.py:45
  69.2 4.4 %collective-permute-done.6 = f32[2,3,1,128,128]{4,3,2,1,0:T(8,128)S(1)} collective-permute-done((f32[2,3,1,128,128]{4,3,2,1,0:T(8,128)S(1)}, f32[2,3,1,128,128]{4,3,2,1,0:T(8,128)S(1)}, u32[]{:S(2)}, u32[]{:S(2)}) %collective-permute-start.6) | collective-permute-done | bytes 393248 | tf_op jit(solution)/shard_map/ppermute | solution.py:23
  73.6 3.2 %collective-permute-done.7 = f32[2,3,1,128,128]{4,3,2,1,0:T(8,128)S(1)} collective-permute-done((f32[2,3,1,128,128]{4,3,2,1,0:T(8,128)S(1)}, f32[2,3,1,128,128]{4,3,2,1,0:T(8,128)S(1)}, u32[]{:S(2)}, u32[]{:S(2)}) %collective-permute-start.7) | collective-permute-done | bytes 393248 | tf_op jit(solution)/shard_map/ppermute | solution.py:22
  76.8 2.4 %multiply_reduce_fusion.10 = (f32[2,4,128,128]{3,2,1,0:T(8,128)S(1)}, f32[2,4,128,128]{3,2,1,0:T(8,128)S(1)}, f32[2,3,4,128,128]{4,3,2,1,0:T(8,128)S(1)}) fusion(f32[2,3,4,128,128]{4,3,2,1,0:T(8,128)S(1)} %subtract_select_fusion.2, f32[2,3,1,128,128]{4,3,2,1,0:T(8,128)S(1)} %collective-permute-done.7, f32[4,128,128]{2,1,0:T(8,128)S(1)} %get-tuple-element.91, ...), kind=kLoop, calls=%fused_computation.100 | loop fusion | flops 7995392 | bytes 12845056 | tf_op jit(solution)/shard_map/reduce_sum | solution.py:45
  81.7 4.4 %collective-permute-done.8 = f32[2,3,1,128,128]{4,3,2,1,0:T(8,128)S(1)} collective-permute-done((f32[2,3,1,128,128]{4,3,2,1,0:T(8,128)S(1)}, f32[2,3,1,128,128]{4,3,2,1,0:T(8,128)S(1)}, u32[]{:S(2)}, u32[]{:S(2)}) %collective-permute-start.8) | collective-permute-done | bytes 393248 | tf_op jit(solution)/shard_map/ppermute | solution.py:23
  86.1 3.2 %collective-permute-done.9 = f32[2,3,1,128,128]{4,3,2,1,0:T(8,128)S(1)} collective-permute-done((f32[2,3,1,128,128]{4,3,2,1,0:T(8,128)S(1)}, f32[2,3,1,128,128]{4,3,2,1,0:T(8,128)S(1)}, u32[]{:S(2)}, u32[]{:S(2)}) %collective-permute-start.9) | collective-permute-done | bytes 393248 | tf_op jit(solution)/shard_map/ppermute | solution.py:22
  89.3 2.6 %multiply_reduce_fusion.8 = (f32[2,4,128,128]{3,2,1,0:T(8,128)S(1)}, f32[2,4,128,128]{3,2,1,0:T(8,128)S(1)}, f32[2,3,4,128,128]{4,3,2,1,0:T(8,128)S(1)}) fusion(f32[2,3,4,128,128]{4,3,2,1,0:T(8,128)S(1)} %subtract_select_fusion.1, f32[2,3,1,128,128]{4,3,2,1,0:T(8,128)S(1)} %collective-permute-done.9, f32[4,128,128]{2,1,0:T(8,128)S(1)} %get-tuple-element.91, ...), kind=kLoop, calls=%fused_computation.98 | loop fusion | flops 7995392 | bytes 12845056 | tf_op jit(solution)/shard_map/reduce_sum | solution.py:45
  94.4 4.4 %collective-permute-done.10 = f32[2,3,1,128,128]{4,3,2,1,0:T(8,128)S(1)} collective-permute-done((f32[2,3,1,128,128]{4,3,2,1,0:T(8,128)S(1)}, f32[2,3,1,128,128]{4,3,2,1,0:T(8,128)S(1)}, u32[]{:S(2)}, u32[]{:S(2)}) %collective-permute-start.10) | collective-permute-done | bytes 393248 | tf_op jit(solution)/shard_map/ppermute | solution.py:23
  98.9 3.2 %collective-permute-done.11 = f32[2,3,1,128,128]{4,3,2,1,0:T(8,128)S(1)} collective-permute-done((f32[2,3,1,128,128]{4,3,2,1,0:T(8,128)S(1)}, f32[2,3,1,128,128]{4,3,2,1,0:T(8,128)S(1)}, u32[]{:S(2)}, u32[]{:S(2)}) %collective-permute-start.11) | collective-permute-done | bytes 393248 | tf_op jit(solution)/shard_map/ppermute | solution.py:22
  102.0 2.1 %multiply_reduce_fusion.6 = (f32[2,4,128,128]{3,2,1,0:T(8,128)S(1)}, f32[2,3,4,128,128]{4,3,2,1,0:T(8,128)S(1)}) fusion(f32[2,3,4,128,128]{4,3,2,1,0:T(8,128)S(1)} %subtract_select_fusion, f32[2,3,1,128,128]{4,3,2,1,0:T(8,128)S(1)} %collective-permute-done.11, f32[4,128,128]{2,1,0:T(8,128)S(1)} %get-tuple-element.91, ...), kind=kLoop, calls=%fused_computation.96 | loop fusion | flops 7340032 | bytes 12320768 | tf_op jit(solution)/shard_map/reduce_sum | solution.py:51
  104.2 0.8 maximum_sqrt_fusion.5
  105.9 0.8 add_select_fusion.1
  108.8 4.4 %collective-permute-done.12 = f32[2,3,1,128,128]{4,3,2,1,0:T(8,128)S(1)} collective-permute-done((f32[2,3,1,128,128]{4,3,2,1,0:T(8,128)S(1)}, f32[2,3,1,128,128]{4,3,2,1,0:T(8,128)S(1)}, u32[]{:S(2)}, u32[]{:S(2)}) %collective-permute-start.12) | collective-permute-done | bytes 393248 | tf_op jit(solution)/shard_map/ppermute | solution.py:23
  113.2 3.2 %collective-permute-done.13 = f32[2,3,1,128,128]{4,3,2,1,0:T(8,128)S(1)} collective-permute-done((f32[2,3,1,128,128]{4,3,2,1,0:T(8,128)S(1)}, f32[2,3,1,128,128]{4,3,2,1,0:T(8,128)S(1)}, u32[]{:S(2)}, u32[]{:S(2)}) %collective-permute-start.13) | collective-permute-done | bytes 393248 | tf_op jit(solution)/shard_map/ppermute | solution.py:22
  116.4 2.2 %multiply_reduce_fusion.3 = (f32[2,4,128,128]{3,2,1,0:T(8,128)S(1)}, f32[2,3,4,128,128]{4,3,2,1,0:T(8,128)S(1)}) fusion(f32[2,3,4,128,128]{4,3,2,1,0:T(8,128)S(1)} %add_select_fusion.1, f32[2,3,1,128,128]{4,3,2,1,0:T(8,128)S(1)} %collective-permute-done.13, f32[4,128,128]{2,1,0:T(8,128)S(1)} %get-tuple-element.91, ...), kind=kLoop, calls=%fused_computation.91 | loop fusion | flops 7340032 | bytes 12320768 | tf_op jit(solution)/shard_map/reduce_sum | solution.py:51
  118.6 0.8 maximum_sqrt_fusion.1
  120.2 0.9 multiply_reduce_fusion
  121.3 0.6 broadcast_in_dim.61
  121.9 4.7 %all-to-all-start = ((f32[32,1,2]{2,1,0:T(1,128)}), f32[32,1,2]{2,1,0:T(1,128)S(1)}, u32[]{:S(2)}, u32[]{:S(2)}) async-start(f32[32,1,2]{2,1,0:T(1,128)} %broadcast_in_dim.61), calls=%async_computation | async-start | bytes 32768 | tf_op jit(solution)/shard_map/all_to_all | solution.py:30
  126.8 1.2 slice_bitcast_fusion.1
  128.1 4.5 %collective-permute-start.14 = (f32[1,3,4,128,128]{4,3,2,1,0:T(8,128)}, f32[1,3,4,128,128]{4,3,2,1,0:T(8,128)}, u32[]{:S(2)}, u32[]{:S(2)}) collective-permute-start(f32[1,3,4,128,128]{4,3,2,1,0:T(8,128)} %get-tuple-element.24), channel_id=1, source_target_pairs={{0,32},{32,64},{64,96},{1,33},{33,65},{65,97},{2,34},{34,66},{66,9... | collective-permute-start | bytes 2359304 | tf_op jit(solution)/shard_map/ppermute | solution.py:41
  132.5 1.3 collective-permute-start.15
  134.0 4.4 %all-to-all-done = f32[32,1,2]{2,1,0:T(1,128)S(1)} async-done(((f32[32,1,2]{2,1,0:T(1,128)}), f32[32,1,2]{2,1,0:T(1,128)S(1)}, u32[]{:S(2)}, u32[]{:S(2)}) %all-to-all-start) | async-done | bytes 288 | tf_op jit(solution)/shard_map/all_to_all | solution.py:30
  138.6 0.6 fusion.82
  139.2 4.0 %collective-permute-start.16 = (f32[1]{0:T(128)}, f32[1]{0:T(128)}, u32[]{:S(2)}, u32[]{:S(2)}) collective-permute-start(f32[1]{0:T(128)} %bitcast.16), channel_id=1, source_target_pairs={{0,32},{32,64},{64,96},{1,33},{33,65},{65,97},{2,34},{34,66},{66,9... | collective-permute-start | bytes 20 | tf_op jit(solution)/shard_map/ppermute | solution.py:41
  143.2 1.3 collective-permute-start.17
  144.5 4.1 %collective-permute-done.16 = f32[1]{0:T(128)} collective-permute-done((f32[1]{0:T(128)}, f32[1]{0:T(128)}, u32[]{:S(2)}, u32[]{:S(2)}) %collective-permute-start.16) | collective-permute-done | bytes 36 | tf_op jit(solution)/shard_map/ppermute | solution.py:41
  148.6 5.1 %collective-permute-done.17 = f32[1]{0:T(128)} collective-permute-done((f32[1]{0:T(128)}, f32[1]{0:T(128)}, u32[]{:S(2)}, u32[]{:S(2)}) %collective-permute-start.17) | collective-permute-done | bytes 36 | tf_op jit(solution)/shard_map/ppermute | solution.py:41
  153.7 1.2 pad_maximum_fusion.17
  155.2 0.6 slice.439
  155.8 1.6 %pad_maximum_fusion = f32[4,3,4,128,128]{4,3,2,1,0:T(8,128)S(1)} fusion(f32[1,3,4,128,128]{4,3,2,1,0:T(8,128)} %collective-permute-done.15, f32[2,3,4,128,128]{4,3,2,1,0:T(8,128)S(1)} %reverse_select_fusion.1, f32[1,3,4,128,128]{4,3,2,1,0:T(8,128)} %collective-permute-done.14), kind=kLoop, calls=%fused_computation.1 | loop fusion | flops 1572864 | bytes 6291456 | tf_op jit(solution)/shard_map/concatenate | solution.py:172
  158.0 1.3 slice.496
  (99 shorter events, 15.9 us)
Async XLA Ops:
  0.6 31.5 %copy-start = (f32[2,3,4,128,128]{4,3,2,1,0:T(8,128)S(1)}, f32[2,3,4,128,128]{4,3,2,1,0:T(8,128)}, u32[]{:S(2)}) copy-start(f32[2,3,4,128,128]{4,3,2,1,0:T(8,128)} %param.8) | copy-start | bytes 4718596
  0.6 25.4 %copy-start.9 = (s32[2]{0:T(128)S(1)}, s32[2]{0:T(128)}, u32[]{:S(2)}) copy-start(s32[2]{0:T(128)} %param.15) | copy-start | bytes 28
  2.2 43.4 %collective-permute-start.2 = (f32[1,1,128,128]{3,2,1,0:T(8,128)}, f32[1,1,128,128]{3,2,1,0:T(8,128)}, u32[]{:S(2)}, u32[]{:S(2)}) collective-permute-start(f32[1,1,128,128]{3,2,1,0:T(8,128)} %slice.366), channel_id=1, source_target_pairs={{0,1},{1,2},{2,3},{3,4},{4,5},{5,6},{6,7},{7,8},{8,9},{9,10},{10,1... | collective-permute-start | bytes 196616 | tf_op jit(solution)/shard_map/ppermute | solution.py:12
  4.2 42.9 %collective-permute-start.1 = (f32[2,3,1,128,128]{4,3,2,1,0:T(8,128)}, f32[2,3,1,128,128]{4,3,2,1,0:T(8,128)}, u32[]{:S(2)}, u32[]{:S(2)}) collective-permute-start(f32[2,3,1,128,128]{4,3,2,1,0:T(8,128)} %get-tuple-element.84), channel_id=1, source_target_pairs={{1,0},{2,1},{3,2},{4,3},{5,4},{6,5},{7,6},{8,7},{9,8},{10,9},{11,1... | collective-permute-start | bytes 1179656 | tf_op jit(solution)/shard_map/ppermute | solution.py:23
  26.1 21.0 %collective-permute-start.3 = (f32[2,3,1,128,128]{4,3,2,1,0:T(8,128)S(1)}, f32[2,3,1,128,128]{4,3,2,1,0:T(8,128)}, u32[]{:S(2)}, u32[]{:S(2)}) collective-permute-start(f32[2,3,1,128,128]{4,3,2,1,0:T(8,128)S(1)} %get-tuple-element.85), channel_id=1, source_target_pairs={{0,1},{1,2},{2,3},{3,4},{4,5},{5,6},{6,7},{7,8},{8,9},{9,10},{10,1... | collective-permute-start | bytes 1179656 | tf_op jit(solution)/shard_map/ppermute | solution.py:22
  27.3 17.6 %collective-permute-start = (f32[1]{0:T(128)}, f32[1]{0:T(128)}, u32[]{:S(2)}, u32[]{:S(2)}) collective-permute-start(f32[1]{0:T(128)} %convert_element_type.6), channel_id=1, source_target_pairs={{0,32},{32,64},{64,96},{1,33},{33,65},{65,97},{2,34},{34,66},{66,9... | collective-permute-start | bytes 20 | tf_op jit(solution)/shard_map/ppermute | solution.py:41
  36.6 4.1 %copy-start.11 = (s32[2]{0:T(128)S(1)}, s32[2]{0:T(128)}, u32[]{:S(2)}) copy-start(s32[2]{0:T(128)} %param.11) | copy-start | bytes 28
  36.6 4.6 %copy-start.1 = (f32[2,4,128,128]{3,2,1,0:T(8,128)S(1)}, f32[2,4,128,128]{3,2,1,0:T(8,128)}, u32[]{:S(2)}) copy-start(f32[2,4,128,128]{3,2,1,0:T(8,128)} %param.13) | copy-start | bytes 1572868
  38.6 7.1 %copy-start.6 = (f32[3,4,128,128]{3,2,1,0:T(8,128)S(1)}, f32[3,4,128,128]{3,2,1,0:T(8,128)}, u32[]{:S(2)}) copy-start(f32[3,4,128,128]{3,2,1,0:T(8,128)} %param.9) | copy-start | bytes 2359300
  41.2 5.9 %copy-start.4 = (f32[2,3,4,128,1]{4,3,2,1,0:T(8,128)S(1)}, f32[2,3,4,128,1]{4,3,2,1,0:T(8,128)}, u32[]{:S(2)}) copy-start(f32[2,3,4,128,1]{4,3,2,1,0:T(8,128)} %get-tuple-element.78) | copy-start | bytes 36868
  41.2 5.9 %copy-start.5 = (f32[2,3,4,128,1]{4,3,2,1,0:T(8,128)S(1)}, f32[2,3,4,128,1]{4,3,2,1,0:T(8,128)}, u32[]{:S(2)}) copy-start(f32[2,3,4,128,1]{4,3,2,1,0:T(8,128)} %get-tuple-element.79) | copy-start | bytes 36868
  45.7 1.4 copy-start.3
  46.7 1.5 copy-start.2
  46.7 1.5 copy-start.8
  53.7 7.4 %collective-permute-start.4 = (f32[2,3,1,128,128]{4,3,2,1,0:T(8,128)S(1)}, f32[2,3,1,128,128]{4,3,2,1,0:T(8,128)S(1)}, u32[]{:S(2)}, u32[]{:S(2)}) collective-permute-start(f32[2,3,1,128,128]{4,3,2,1,0:T(8,128)S(1)} %get-tuple-element.74), channel_id=1, source_target_pairs={{1,0},{2,1},{3,2},{4,3},{5,4},{6,5},{7,6},{8,7},{9,8},{10,9},{11,1... | collective-permute-start | bytes 1179656 | tf_op jit(solution)/shard_map/ppermute | solution.py:23
  55.9 8.4 %collective-permute-start.5 = (f32[2,3,1,128,128]{4,3,2,1,0:T(8,128)S(1)}, f32[2,3,1,128,128]{4,3,2,1,0:T(8,128)S(1)}, u32[]{:S(2)}, u32[]{:S(2)}) collective-permute-start(f32[2,3,1,128,128]{4,3,2,1,0:T(8,128)S(1)} %get-tuple-element.75), channel_id=1, source_target_pairs={{0,1},{1,2},{2,3},{3,4},{4,5},{5,6},{6,7},{7,8},{8,9},{9,10},{10,1... | collective-permute-start | bytes 1179656 | tf_op jit(solution)/shard_map/ppermute | solution.py:22
  68.2 5.4 %collective-permute-start.6 = (f32[2,3,1,128,128]{4,3,2,1,0:T(8,128)S(1)}, f32[2,3,1,128,128]{4,3,2,1,0:T(8,128)S(1)}, u32[]{:S(2)}, u32[]{:S(2)}) collective-permute-start(f32[2,3,1,128,128]{4,3,2,1,0:T(8,128)S(1)} %get-tuple-element.64), channel_id=1, source_target_pairs={{1,0},{2,1},{3,2},{4,3},{5,4},{6,5},{7,6},{8,7},{9,8},{10,9},{11,1... | collective-permute-start | bytes 1179656 | tf_op jit(solution)/shard_map/ppermute | solution.py:23
  68.3 8.5 %collective-permute-start.7 = (f32[2,3,1,128,128]{4,3,2,1,0:T(8,128)S(1)}, f32[2,3,1,128,128]{4,3,2,1,0:T(8,128)S(1)}, u32[]{:S(2)}, u32[]{:S(2)}) collective-permute-start(f32[2,3,1,128,128]{4,3,2,1,0:T(8,128)S(1)} %get-tuple-element.65), channel_id=1, source_target_pairs={{0,1},{1,2},{2,3},{3,4},{4,5},{5,6},{6,7},{7,8},{8,9},{9,10},{10,1... | collective-permute-start | bytes 1179656 | tf_op jit(solution)/shard_map/ppermute | solution.py:22
  80.8 5.4 %collective-permute-start.8 = (f32[2,3,1,128,128]{4,3,2,1,0:T(8,128)S(1)}, f32[2,3,1,128,128]{4,3,2,1,0:T(8,128)S(1)}, u32[]{:S(2)}, u32[]{:S(2)}) collective-permute-start(f32[2,3,1,128,128]{4,3,2,1,0:T(8,128)S(1)} %get-tuple-element.54), channel_id=1, source_target_pairs={{1,0},{2,1},{3,2},{4,3},{5,4},{6,5},{7,6},{8,7},{9,8},{10,9},{11,1... | collective-permute-start | bytes 1179656 | tf_op jit(solution)/shard_map/ppermute | solution.py:23
  80.8 8.5 %collective-permute-start.9 = (f32[2,3,1,128,128]{4,3,2,1,0:T(8,128)S(1)}, f32[2,3,1,128,128]{4,3,2,1,0:T(8,128)S(1)}, u32[]{:S(2)}, u32[]{:S(2)}) collective-permute-start(f32[2,3,1,128,128]{4,3,2,1,0:T(8,128)S(1)} %get-tuple-element.55), channel_id=1, source_target_pairs={{0,1},{1,2},{2,3},{3,4},{4,5},{5,6},{6,7},{7,8},{8,9},{9,10},{10,1... | collective-permute-start | bytes 1179656 | tf_op jit(solution)/shard_map/ppermute | solution.py:22
  93.5 5.4 %collective-permute-start.10 = (f32[2,3,1,128,128]{4,3,2,1,0:T(8,128)S(1)}, f32[2,3,1,128,128]{4,3,2,1,0:T(8,128)S(1)}, u32[]{:S(2)}, u32[]{:S(2)}) collective-permute-start(f32[2,3,1,128,128]{4,3,2,1,0:T(8,128)S(1)} %get-tuple-element.44), channel_id=1, source_target_pairs={{1,0},{2,1},{3,2},{4,3},{5,4},{6,5},{7,6},{8,7},{9,8},{10,9},{11,1... | collective-permute-start | bytes 1179656 | tf_op jit(solution)/shard_map/ppermute | solution.py:23
  93.6 8.5 %collective-permute-start.11 = (f32[2,3,1,128,128]{4,3,2,1,0:T(8,128)S(1)}, f32[2,3,1,128,128]{4,3,2,1,0:T(8,128)S(1)}, u32[]{:S(2)}, u32[]{:S(2)}) collective-permute-start(f32[2,3,1,128,128]{4,3,2,1,0:T(8,128)S(1)} %get-tuple-element.45), channel_id=1, source_target_pairs={{0,1},{1,2},{2,3},{3,4},{4,5},{5,6},{6,7},{7,8},{8,9},{9,10},{10,1... | collective-permute-start | bytes 1179656 | tf_op jit(solution)/shard_map/ppermute | solution.py:22
  102.0 2.1 %copy-start.7 = (f32[2,4,128,128]{3,2,1,0:T(8,128)S(1)}, f32[2,4,128,128]{3,2,1,0:T(8,128)}, u32[]{:S(2)}) copy-start(f32[2,4,128,128]{3,2,1,0:T(8,128)} %param.12) | copy-start | bytes 1572868
  102.0 2.1 %copy-start.10 = (f32[2]{0:T(128)S(1)}, f32[2]{0:T(128)}, u32[]{:S(2)}) copy-start(f32[2]{0:T(128)} %param.10) | copy-start | bytes 28
  107.9 5.4 %collective-permute-start.12 = (f32[2,3,1,128,128]{4,3,2,1,0:T(8,128)S(1)}, f32[2,3,1,128,128]{4,3,2,1,0:T(8,128)S(1)}, u32[]{:S(2)}, u32[]{:S(2)}) collective-permute-start(f32[2,3,1,128,128]{4,3,2,1,0:T(8,128)S(1)} %get-tuple-element.34), channel_id=1, source_target_pairs={{1,0},{2,1},{3,2},{4,3},{5,4},{6,5},{7,6},{8,7},{9,8},{10,9},{11,1... | collective-permute-start | bytes 1179656 | tf_op jit(solution)/shard_map/ppermute | solution.py:23
  107.9 8.5 %collective-permute-start.13 = (f32[2,3,1,128,128]{4,3,2,1,0:T(8,128)S(1)}, f32[2,3,1,128,128]{4,3,2,1,0:T(8,128)S(1)}, u32[]{:S(2)}, u32[]{:S(2)}) collective-permute-start(f32[2,3,1,128,128]{4,3,2,1,0:T(8,128)S(1)} %get-tuple-element.35), channel_id=1, source_target_pairs={{0,1},{1,2},{2,3},{3,4},{4,5},{5,6},{6,7},{7,8},{8,9},{9,10},{10,1... | collective-permute-start | bytes 1179656 | tf_op jit(solution)/shard_map/ppermute | solution.py:22
  121.9 16.5 %all-to-all-start = ((f32[32,1,2]{2,1,0:T(1,128)}), f32[32,1,2]{2,1,0:T(1,128)S(1)}, u32[]{:S(2)}, u32[]{:S(2)}) async-start(f32[32,1,2]{2,1,0:T(1,128)} %broadcast_in_dim.61), calls=%async_computation | async-start | bytes 32768 | tf_op jit(solution)/shard_map/all_to_all | solution.py:30
  128.1 27.7 %collective-permute-start.14 = (f32[1,3,4,128,128]{4,3,2,1,0:T(8,128)}, f32[1,3,4,128,128]{4,3,2,1,0:T(8,128)}, u32[]{:S(2)}, u32[]{:S(2)}) collective-permute-start(f32[1,3,4,128,128]{4,3,2,1,0:T(8,128)} %get-tuple-element.24), channel_id=1, source_target_pairs={{0,32},{32,64},{64,96},{1,33},{33,65},{65,97},{2,34},{34,66},{66,9... | collective-permute-start | bytes 2359304 | tf_op jit(solution)/shard_map/ppermute | solution.py:41
  132.5 23.3 %collective-permute-start.15 = (f32[1,3,4,128,128]{4,3,2,1,0:T(8,128)}, f32[1,3,4,128,128]{4,3,2,1,0:T(8,128)}, u32[]{:S(2)}, u32[]{:S(2)}) collective-permute-start(f32[1,3,4,128,128]{4,3,2,1,0:T(8,128)} %get-tuple-element.25), channel_id=1, source_target_pairs={{32,0},{64,32},{96,64},{33,1},{65,33},{97,65},{34,2},{66,34},{98,6... | collective-permute-start | bytes 2359304 | tf_op jit(solution)/shard_map/ppermute | solution.py:41
  139.2 9.4 %collective-permute-start.16 = (f32[1]{0:T(128)}, f32[1]{0:T(128)}, u32[]{:S(2)}, u32[]{:S(2)}) collective-permute-start(f32[1]{0:T(128)} %bitcast.16), channel_id=1, source_target_pairs={{0,32},{32,64},{64,96},{1,33},{33,65},{65,97},{2,34},{34,66},{66,9... | collective-permute-start | bytes 20 | tf_op jit(solution)/shard_map/ppermute | solution.py:41
  143.2 10.5 %collective-permute-start.17 = (f32[1]{0:T(128)}, f32[1]{0:T(128)}, u32[]{:S(2)}, u32[]{:S(2)}) collective-permute-start(f32[1]{0:T(128)} %bitcast.17), channel_id=1, source_target_pairs={{32,0},{64,32},{96,64},{33,1},{65,33},{97,65},{34,2},{66,34},{98,6... | collective-permute-start | bytes 20 | tf_op jit(solution)/shard_map/ppermute | solution.py:41
where the time goes:
time: 160 us; the launch traced here: 159 us
  waiting for transfers between devices  52 us (32%)
  starting transfers between devices  46.9 us (29%)
  other arithmetic  31.8 us (20%)
  local copies, waits for them, and re-layouts  24.7 us (15%)
  between operations  3.87 us (2%)
    ppermute x6, starting transfers between devices, extended(): after = lax.ppermute(leading, axis, down)  24.3 us
    ppermute x6, waiting for transfers between devices, extended(): after = lax.ppermute(leading, axis, down)  22.6 us
    ppermute x5, starting transfers between devices, shifted(): return lax.ppermute(block, axis, route)  15.9 us
    ppermute x6, waiting for transfers between devices, extended(): before = lax.ppermute(last, axis, up)  15.8 us
    reduce_sum x4, other arithmetic, reflect(): projection = jnp.sum(current * pulled, axis=1, keepdims=True)  11.2 us
    slice x12, local copies, waits for them, and re-layouts, local_pull(): jnp.roll(middle, -1, 4)  9.93 us
    ppermute x5, waiting for transfers between devices, shifted(): return lax.ppermute(block, axis, route)  9.21 us
    all_to_all x1, starting transfers between devices, copy_for_each(): return lax.all_to_all(copies, axis, split_axis=0, concat_axis=0, tiled=True)  4.72 us
  transfers between devices with their start and end apart: 19, of which 13 were waited for; matrix products, arithmetic and copies ran while one was open for 14% of the time, Pallas kernels for 0%

commit v1 on v0

v1 whole, which is shorter than its diff:
```python
import functools

import jax
import jax.numpy as jnp
from jax import lax
from jax.experimental import pallas as pl
from jax.experimental.pallas import tpu as pltpu
from jax.sharding import PartitionSpec as P

OR_SWEEPS = 2
OR_HALVES = 2 * OR_SWEEPS
HALVES = OR_HALVES + 2
PAD = 8
MESH = pl.DeviceIdType.MESH

SIN_TERMS = (
    1.0,
    -1.0 / 6,
    1.0 / 120,
    -1.0 / 5040,
    1.0 / 362880,
    -1.0 / 39916800,
    1.0 / 6227020800,
)
COS_TERMS = (
    1.0,
    -1.0 / 2,
    1.0 / 24,
    -1.0 / 720,
    1.0 / 40320,
    -1.0 / 3628800,
    1.0 / 479001600,
    -1.0 / 87178291200,
)


def series(terms, square):
    total = jnp.full_like(square, terms[-1])
    for term in terms[-2::-1]:
        total = total * square + term
    return total


def cos_sin(angle):
    half = 0.5 * angle
    square = half * half
    sine = half * series(SIN_TERMS, square)
    cosine = series(COS_TERMS, square)
    return 1.0 - 2.0 * sine * sine, 2.0 * sine * cosine


def sweep_kernel(
    spin_hbm,
    bond_hbm,
    level_hbm,
    height_hbm,
    angle_hbm,
    beta_ref,
    order_ref,
    bits_ref,
    out_ref,
    energy_ref,
    spin_in,
    bond_in,
    heat_in,
    state,
    bond_x,
    bond_yo,
    bond_ys,
    bond_z,
    bond_halo,
    trial,
    load_sem,
    bond_send,
    bond_recv,
    send_sem,
    recv_sem,
):
    planes, rows, columns = spin_in.shape[2:]
    half = rows // 2
    chunk = min(16, half)
    me = lax.axis_index("gz")
    count = lax.axis_size("gz")
    upper = lax.rem(me + 1, count)
    lower = lax.rem(me + count - 1, count)
    main = pl.ds(PAD, half)

    loads = [
        pltpu.make_async_copy(spin_hbm, spin_in, load_sem.at[0]),
        pltpu.make_async_copy(bond_hbm, bond_in, load_sem.at[1]),
        pltpu.make_async_copy(level_hbm, heat_in.at[0], load_sem.at[2]),
        pltpu.make_async_copy(height_hbm, heat_in.at[1], load_sem.at[3]),
        pltpu.make_async_copy(angle_hbm, heat_in.at[2], load_sem.at[4]),
    ]
    for load in loads:
        load.start()

    barrier = pltpu.get_barrier_semaphore()
    for neighbour in (lower, upper):
        pl.semaphore_signal(
            barrier, inc=1, device_id={"gz": neighbour}, device_id_type=MESH
        )

    lane = lax.broadcasted_iota(jnp.int32, (half, columns), 1) % 2
    lane_chunk = lax.broadcasted_iota(jnp.int32, (chunk, columns), 1) % 2
    swapped = bits_ref[0] != 0

    def order_of(slot):
        other = 1 - slot
        return jnp.where(swapped, order_ref[other], order_ref[slot])

    def beta_of(slot):
        other = 1 - slot
        return jnp.where(swapped, beta_ref[other], beta_ref[slot])

    def parity(slot, plane):
        return lax.rem(me * planes + plane + order_of(slot), 2)

    def upward(step, slot):
        return pltpu.make_async_remote_copy(
            src_ref=state.at[step, slot, planes, :, main],
            dst_ref=state.at[step, slot, 0, :, main],
            send_sem=send_sem.at[step, slot, 0],
            recv_sem=recv_sem.at[step, slot, 0],
            device_id={"gz": upper},
            device_id_type=MESH,
        )

    def downward(step, slot):
        return pltpu.make_async_remote_copy(
            src_ref=state.at[step, slot, 1, :, main],
            dst_ref=state.at[step, slot, planes + 1, :, main],
            send_sem=send_sem.at[step, slot, 1],
            recv_sem=recv_sem.at[step, slot, 1],
            device_id={"gz": lower},
            device_id_type=MESH,
        )

    bond_up = pltpu.make_async_remote_copy(
        src_ref=bond_in.at[2, planes - 1],
        dst_ref=bond_halo,
        send_sem=bond_send,
        recv_sem=bond_recv,
        device_id={"gz": upper},
        device_id_type=MESH,
    )

    even_rows = pl.ds(0, half, stride=2)
    odd_rows = pl.ds(1, half, stride=2)

    def wrap_rows(step, slot, plane):
        for part in range(3):
            state[step, slot, plane, part, PAD - 1 : PAD] = state[
                step, slot, plane, part, PAD + half - 1 : PAD + half
            ]
            state[step, slot, plane, part, PAD + half : PAD + half + 1] = state[
                step, slot, plane, part, PAD : PAD + 1
            ]

    def pack_spins(plane, _):
        for part in range(3):
            pairs = [
                (spin_in[r, part, plane, even_rows, :], spin_in[r, part, plane, odd_rows, :])
                for r in (0, 1)
            ]
            for slot in (0, 1):
                even = jnp.where(swapped, pairs[1 - slot][0], pairs[slot][0])
                odd = jnp.where(swapped, pairs[1 - slot][1], pairs[slot][1])
                mask = lane == parity(slot, plane)
                state[0, slot, plane + 1, part, main] = jnp.where(mask, even, odd)
                state[1, slot, plane + 1, part, main] = jnp.where(mask, odd, even)
        for slot in (0, 1):
            wrap_rows(1, slot, plane + 1)
            wrap_rows(0, slot, plane + 1)
        return 0

    loads[0].wait()
    lax.fori_loop(0, planes, pack_spins, 0)
    loads[1].wait()

    pl.semaphore_wait(barrier, 2)
    for slot in (0, 1):
        upward(1, slot).start()
        downward(1, slot).start()
    bond_up.start()

    def pack_bonds(plane, _):
        even, odd = bond_in[0, plane, even_rows, :], bond_in[0, plane, odd_rows, :]
        first = jnp.where(lane == 0, even, odd)
        second = jnp.where(lane == 0, odd, even)
        bond_x[0, plane, 0] = first
        bond_x[1, plane, 0] = second
        bond_x[0, plane, 1] = pltpu.roll(second, 1, 1)
        bond_x[1, plane, 1] = pltpu.roll(first, 1, 1)
        even, odd = bond_in[1, plane, even_rows, :], bond_in[1, plane, odd_rows, :]
        before = pltpu.roll(odd, 1, 0)
        bond_ys[plane] = even
        bond_yo[0, plane] = jnp.where(lane == 0, before, odd)
        bond_yo[1, plane] = jnp.where(lane == 0, odd, before)
        even, odd = bond_in[2, plane, even_rows, :], bond_in[2, plane, odd_rows, :]
        bond_z[0, plane + 1] = jnp.where(lane == 0, even, odd)
        bond_z[1, plane + 1] = jnp.where(lane == 0, odd, even)
        return 0

    lax.fori_loop(0, planes, pack_bonds, 0)
    bond_up.wait_recv()
    even, odd = bond_halo[even_rows, :], bond_halo[odd_rows, :]
    bond_z[0, 0] = jnp.where(lane == 0, even, odd)
    bond_z[1, 0] = jnp.where(lane == 0, odd, even)

    for load in loads[2:]:
        load.wait()

    def pack_heat(slot, plane):
        side = 1 - slot
        mask = lane_chunk == parity(slot, plane)
        for start in range(0, half, chunk):
            here = pl.ds(start, chunk)
            even_here = pl.ds(2 * start, chunk, stride=2)
            odd_here = pl.ds(2 * start + 1, chunk, stride=2)
            draws = []
            for kind in range(3):
                even = jnp.where(
                    swapped,
                    heat_in[kind, side, plane, even_here, :],
                    heat_in[kind, slot, plane, even_here, :],
                )
                odd = jnp.where(
                    swapped,
                    heat_in[kind, side, plane, odd_here, :],
                    heat_in[kind, slot, plane, odd_here, :],
                )
                draws.append((jnp.where(mask, even, odd), jnp.where(mask, odd, even)))
            for colour in (0, 1):
                level, height, angle = (draw[colour] for draw in draws)
                across = jnp.sqrt(jnp.maximum(1.0 - height * height, 0.0))
                cosine, sine = cos_sin(angle)
                trial[slot, colour, plane, 0, here] = level
                trial[slot, colour, plane, 1, here] = across * cosine
                trial[slot, colour, plane, 2, here] = across * sine
                trial[slot, colour, plane, 3, here] = height

    def pulls(step, slot, plane, pattern, mask, start):
        here = pl.ds(start, chunk)
        east, west = bond_x[pattern, plane - 1, 0, here], bond_x[pattern, plane - 1, 1, here]
        near, far = bond_ys[plane - 1, here], bond_yo[pattern, plane - 1, here]
        above, below = bond_z[pattern, plane, here], bond_z[pattern, plane - 1, here]
        at = pl.ds(PAD + start, chunk)
        out = []
        for part in range(3):
            centre = state[step, slot, plane, part, at]
            other = jnp.where(
                mask,
                state[step, slot, plane, part, pl.ds(PAD + start - 1, chunk)],
                state[step, slot, plane, part, pl.ds(PAD + start + 1, chunk)],
            )
            pulled = east * pltpu.roll(centre, columns - 1, 1) + west * pltpu.roll(centre, 1, 1)
            pulled = pulled + near * centre + far * other
            pulled = pulled + above * state[step, slot, plane + 1, part, at]
            pulled = pulled + below * state[step, slot, plane - 1, part, at]
            out.append(pulled)
        return out

    def dot(first, second):
        return first[0] * second[0] + first[1] * second[1] + first[2] * second[2]

    def relax_plane(step, slot, plane):
        pattern = lax.rem(parity(slot, plane - 1) + step + 1, 2)
        mask = lane_chunk == pattern
        for start in range(0, half, chunk):
            at = pl.ds(PAD + start, chunk)
            pulled = pulls(step, slot, plane, pattern, mask, start)
            old = [state[step - 1, slot, plane, part, at] for part in range(3)]
            scale = 2.0 * dot(old, pulled) / jnp.maximum(dot(pulled, pulled), 0.01)
            for part in range(3):
                state[step + 1, slot, plane, part, at] = scale * pulled[part] - old[part]
        wrap_rows(step + 1, slot, plane)

    def heat_plane(step, slot, plane):
        colour = step - OR_HALVES - 1
        pattern = lax.rem(parity(slot, plane - 1) + step + 1, 2)
        mask = lane_chunk == pattern
        beta = beta_of(slot)
        gain = jnp.zeros((8, columns), jnp.float32)
        for start in range(0, half, chunk):
            at = pl.ds(PAD + start, chunk)
            here = pl.ds(start, chunk)
            pulled = pulls(step, slot, plane, pattern, mask, start)
            square = jnp.maximum(dot(pulled, pulled), 0.01)
            inverse = lax.rsqrt(square)
            reach = beta * (square * inverse)
            axis = [part * inverse for part in pulled]
            level = trial[slot, colour, plane - 1, 0, here]
            cosine = 1.0 + jnp.log((1.0 - level) + level * jnp.exp(-2.0 * reach)) / reach
            draw = [trial[slot, colour, plane - 1, part, here] for part in (1, 2, 3)]
            along = dot(draw, axis)
            tangent = [draw[part] - along * axis[part] for part in range(3)]
            norm = lax.rsqrt(jnp.maximum(dot(tangent, tangent), 0.0001))
            side = jnp.sqrt(jnp.maximum(1.0 - cosine * cosine, 0.0)) * norm
            fresh = [cosine * axis[part] + side * tangent[part] for part in range(3)]
            for part in range(3):
                state[step + 1, slot, plane, part, at] = fresh[part]
            gain = gain + jnp.sum(dot(fresh, pulled).reshape(-1, 8, columns), axis=0)
        wrap_rows(step + 1, slot, plane)
        return gain

    def boundary_first(index):
        return jnp.where(index == 0, 1, jnp.where(index == 1, planes, index))

    def halves(step, slot, body, send, initial):
        def visit(index, carry):
            plane = boundary_first(index)

            @pl.when(index == 0)
            def _():
                upward(step, slot).wait_recv()

            @pl.when(index == 1)
            def _():
                downward(step, slot).wait_recv()

            carry = body(step, slot, plane, carry)
            if send:

                @pl.when(index == 0)
                def _():
                    downward(step + 1, slot).start()

                @pl.when(index == 1)
                def _():
                    upward(step + 1, slot).start()

            return carry

        return lax.fori_loop(0, planes, visit, initial)

    def relax_body(step, slot, plane, carry):
        relax_plane(step, slot, plane)
        return carry

    def heat_body(step, slot, plane, carry):
        return carry + heat_plane(step, slot, plane)

    def relax_round(visit, _):
        step = visit // 2 + 1
        slot = lax.rem(visit, 2)
        halves(step, slot, relax_body, True, 0)
        share = planes // OR_HALVES

        def fill(index, _):
            pack_heat_dynamic(slot, (step - 1) * share + index)
            return 0

        lax.fori_loop(0, share, fill, 0)
        return 0

    def pack_heat_dynamic(slot, plane):
        pack_heat(slot, plane)

    lax.fori_loop(0, 2 * OR_HALVES, relax_round, 0)

    for step in (OR_HALVES + 1, OR_HALVES + 2):
        last = step == OR_HALVES + 2

        def heat_round(slot, _, step=step, last=last):
            zero = jnp.zeros((8, columns), jnp.float32)
            gain = halves(step, slot, heat_body, not last, zero)
            if last:
                energy_ref[slot] = gain
            return 0

        lax.fori_loop(0, 2, heat_round, 0)

    def unpack(plane, _):
        for slot in (0, 1):
            mask = lane == parity(slot, plane)
            for part in range(3):
                first = state[HALVES, slot, plane + 1, part, main]
                second = state[HALVES + 1, slot, plane + 1, part, main]
                out_ref[slot, part, plane, even_rows, :] = jnp.where(mask, first, second)
                out_ref[slot, part, plane, odd_rows, :] = jnp.where(mask, second, first)
        return 0

    lax.fori_loop(0, planes, unpack, 0)

    bond_up.wait_send()

    def drain(index, _):
        step = index // 2 + 1
        slot = lax.rem(index, 2)
        upward(step, slot).wait_send()
        downward(step, slot).wait_send()
        return 0

    lax.fori_loop(0, 2 * HALVES, drain, 0)


def sweep(spin_state, couplings, level, height, angle, beta, order, bits):
    slots, parts, planes, rows, columns = spin_state.shape
    half = rows // 2
    f32 = jnp.float32
    any_space = pl.BlockSpec(memory_space=pl.ANY)
    smem = pl.BlockSpec(memory_space=pltpu.SMEM)
    vmem = pl.BlockSpec(memory_space=pltpu.VMEM)
    return pl.pallas_call(
        sweep_kernel,
        out_shape=(
            jax.ShapeDtypeStruct(spin_state.shape, f32),
            jax.ShapeDtypeStruct((slots, 8, columns), f32),
        ),
        in_specs=[any_space] * 5 + [smem] * 3,
        out_specs=(vmem, vmem),
        scratch_shapes=[
            pltpu.VMEM(spin_state.shape, f32),
            pltpu.VMEM(couplings.shape, f32),
            pltpu.VMEM((3,) + level.shape, f32),
            pltpu.VMEM((HALVES + 2, slots, planes + 2, 3, half + 2 * PAD, columns), f32),
            pltpu.VMEM((2, planes, 2, half, columns), f32),
            pltpu.VMEM((2, planes, half, columns), f32),
            pltpu.VMEM((planes, half, columns), f32),
            pltpu.VMEM((2, planes + 1, half, columns), f32),
            pltpu.VMEM((rows, columns), f32),
            pltpu.VMEM((slots, 2, planes, 4, half, columns), f32),
            pltpu.SemaphoreType.DMA((5,)),
            pltpu.SemaphoreType.DMA,
            pltpu.SemaphoreType.DMA,
            pltpu.SemaphoreType.DMA((HALVES + 1, slots, 2)),
            pltpu.SemaphoreType.DMA((HALVES + 1, slots, 2)),
        ],
        compiler_params=pltpu.CompilerParams(
            collective_id=0, has_side_effects=True, vmem_limit_bytes=56 * 1024 * 1024
        ),
        name="sweep",
    )(spin_state, couplings, level, height, angle, beta, order, bits)


def copy_for_each(array, axis):
    copies = jnp.broadcast_to(array, (lax.axis_size(axis), *array.shape))
    return lax.all_to_all(copies, axis, split_axis=0, concat_axis=0, tiled=True)


def of_everyone(array, axis):
    return jnp.sum(copy_for_each(array, axis), axis=0)


def shifted(block, axis, distance):
    devices = range(lax.axis_size(axis))
    route = [(i - distance, i) for i in devices if i - distance in devices]
    return lax.ppermute(block, axis, route)


def on_device(
    spin_state,
    couplings,
    inverse_temps,
    colour_order,
    heat_level,
    heat_height,
    heat_angle,
    swap_bits,
):
    planes, rows, columns = spin_state.shape[2:]
    spin_now, gains = sweep(
        spin_state,
        couplings,
        heat_level,
        heat_height,
        heat_angle,
        inverse_temps,
        colour_order,
        swap_bits,
    )
    total_sites = float(columns * rows * planes * lax.axis_size("gz"))
    energy_now = of_everyone(-jnp.sum(gains, axis=(1, 2)), "gz") / total_sites
    below_spin, below_energy, below_bit = shifted(
        (spin_now[1:], energy_now[1:], swap_bits[1:].astype(jnp.float32)), "temp", 1
    )
    above_spin, above_energy = shifted((spin_now[:1], energy_now[:1]), "temp", -1)
    top_device = lax.axis_index("temp") == lax.axis_size("temp") - 1
    take_below = below_bit[0] > 0.5
    take_above = (swap_bits[1] != 0) & ~top_device
    spin_final = jnp.concatenate(
        [
            jnp.where(take_below, below_spin, spin_now[:1]),
            jnp.where(take_above, above_spin, spin_now[1:]),
        ]
    )
    energies = jnp.concatenate(
        [
            jnp.where(take_below, below_energy, energy_now[:1]),
            jnp.where(take_above, above_energy, energy_now[1:]),
        ]
    )
    return (spin_final, energies)


def solution(mesh):
    return jax.shard_map(
        on_device,
        mesh=mesh,
        in_specs=(
            P(("group", "temp"), None, "gz", None, None),
            P(None, ("group", "gz"), None, None),
            P(("group", "temp")),
            P(("group", "temp")),
            P(("group", "temp"), "gz", None, None),
            P(("group", "temp"), "gz", None, None),
            P(("group", "temp"), "gz", None, None),
            P(("group", "temp")),
        ),
        out_specs=(P(("group", "temp"), None, "gz", None, None), P(("group", "temp"))),
        check_vma=False,
    )
```

time: 160 us -> 91.6 us (0.57)
  Pallas kernels: 0 us -> 51.1 us
  waiting for transfers between devices: 52 us -> 3.66 us
  other arithmetic: 31.8 us -> 2.19 us
  starting transfers between devices: 46.9 us -> 24.5 us
  local copies, waits for them, and re-layouts: 24.7 us -> 4.59 us
    pallas_call x0 -> x1, Pallas kernels: none -> 51.1 us  [sweep(): pl.pallas_call(sweep_kernel, out_shape=(jax.ShapeDtypeStruct(spin_state.s...]
    ppermute x13 -> x0, waiting for transfers between devices: 38.4 us -> none  [the longest x6 22.6 us: extended(): after = lax.ppermute(leading, axis, down)]
    ppermute x13 -> x0, starting transfers between devices: 26.2 us -> none  [the longest x6 24.3 us: extended(): after = lax.ppermute(leading, axis, down)]
    slice x38 -> x3, local copies, waits for them, and re-layouts: 22.5 us -> 3.96 us  [the longest x1 2.78 us: on_device(): spin_now[1:]]
    reduce_sum x13 -> x2, other arithmetic: 18.1 us -> 0.15 us  [the longest x1 0.1 us: on_device(): energy_now = of_everyone(-jnp.sum(gains, axis=(1, 2)), 'gz') / total_sites]
    ppermute x5, waiting for transfers between devices: 9.21 us -> 2.88 us  [shifted(): return lax.ppermute(block, axis, route)]
    mul x2 -> x0, other arithmetic: 4.78 us -> none  [the longest x1 3.73 us: heat_bath(): side * jnp.cos(angle_draw)]
    ppermute x5, starting transfers between devices: 15.9 us -> 19.6 us  [shifted(): return lax.ppermute(block, axis, route)]
  transfers between devices with their start and end apart: 19 -> 6, of which waited for: 13 -> 2; matrix products, arithmetic and copies ran while one was open for 14% -> 3% of each run, Pallas kernels for 0% -> 0%
where the time goes in v1:
time: 91.6 us; the launch traced here: 91.3 us
  Pallas kernels  51.1 us (56%)
  starting transfers between devices  24.5 us (27%)
  between operations  5.24 us (6%)
  local copies, waits for them, and re-layouts  4.59 us (5%)
  waiting for transfers between devices  3.66 us (4%)
  other arithmetic  2.19 us (2%)
    pallas_call x1, Pallas kernels, sweep(): pl.pallas_call(sweep_kernel, out_shape=(jax.ShapeDtypeStruct(spin_state.s...  51.1 us
    ppermute x5, starting transfers between devices, shifted(): return lax.ppermute(block, axis, route)  19.6 us
    all_to_all x1, starting transfers between devices, copy_for_each(): return lax.all_to_all(copies, axis, split_axis=0, concat_axis=0, tiled=True)  4.94 us
    ppermute x5, waiting for transfers between devices, shifted(): return lax.ppermute(block, axis, route)  2.88 us
    slice x1, local copies, waits for them, and re-layouts, on_device(): spin_now[1:]  2.78 us
  transfers between devices with their start and end apart: 6, of which 2 were waited for; matrix products, arithmetic and copies ran while one was open for 3% of the time, Pallas kernels for 0%

profile of v1, /device:TPU:40, one launch (start us, length us, event | category | flops | bytes accessed | tf_op | source)
XLA Modules:
  0.0 91.3 jit_solution(10666178790057065196)
XLA Ops:
  0.6 51.1 %sweep.1 = (f32[2,3,4,128,128]{4,3,2,1,0:T(8,128)}, f32[2,8,128]{2,1,0:T(8,128)}) custom-call(f32[2,3,4,128,128]{4,3,2,1,0:T(8,128)} %spin_hbm.1, f32[3,4,128,128]{3,2,1,0:T(8,128)} %bond_hbm.1, f32[2,4,128,128]{3,2,1,0:T(8,128)} %level_hbm.1, f32[2,4,128,128]{3,2,1,0:T(8,128)} %height_hbm.1, f32[2,4,128,128]{3,2,1,0:T(8,128)} %angle_hbm.1, f32[2]{0:T(128)} %beta_ref.1, ...), custom_call_target="tpu_custom_call" | custom-call | tf_op jit(solution)/shard_map/sweep/pallas_call | solution.py:405
  51.8 0.0 copy-start.1
  51.8 0.0 copy-start.2
  51.8 0.0 copy-start
  51.8 2.8 %fusion = (f32[1,3,4,128,128]{4,3,2,1,0:T(8,128)}, f32[1,3,4,128,128]{4,3,2,1,0:T(8,128)}) fusion(f32[2,3,4,128,128]{4,3,2,1,0:T(8,128)} %get-tuple-element.4), kind=kLoop, calls=%fused_computation.5 | loop fusion | bytes 3145728 | tf_op jit(solution)/shard_map/slice | solution.py:476
  54.6 3.6 %collective-permute-start.1 = (f32[1,3,4,128,128]{4,3,2,1,0:T(8,128)}, f32[1,3,4,128,128]{4,3,2,1,0:T(8,128)S(1)}, u32[]{:S(2)}, u32[]{:S(2)}) collective-permute-start(f32[1,3,4,128,128]{4,3,2,1,0:T(8,128)} %get-tuple-element.8), channel_id=1, source_target_pairs={{0,32},{32,64},{64,96},{1,33},{33,65},{65,97},{2,34},{34,66},{66,9... | collective-permute-start | bytes 2359304 | tf_op jit(solution)/shard_map/ppermute | solution.py:449
  58.2 1.3 %collective-permute-start.2 = (f32[1,3,4,128,128]{4,3,2,1,0:T(8,128)}, f32[1,3,4,128,128]{4,3,2,1,0:T(8,128)S(1)}, u32[]{:S(2)}, u32[]{:S(2)}) collective-permute-start(f32[1,3,4,128,128]{4,3,2,1,0:T(8,128)} %get-tuple-element.9), channel_id=1, source_target_pairs={{32,0},{64,32},{96,64},{33,1},{65,33},{97,65},{34,2},{66,34},{98,6... | collective-permute-start | bytes 2359304 | tf_op jit(solution)/shard_map/ppermute | solution.py:449
  59.5 0.0 copy-done.1
  59.5 0.1 reduce_sum.18
  59.6 0.6 broadcast_in_dim.3
  60.2 4.9 %all-to-all-start = ((f32[32,1,2]{2,1,0:T(1,128)}), f32[32,1,2]{2,1,0:T(1,128)S(1)}, u32[]{:S(2)}, u32[]{:S(2)}) async-start(f32[32,1,2]{2,1,0:T(1,128)} %broadcast_in_dim.3), calls=%async_computation | async-start | bytes 32768 | tf_op jit(solution)/shard_map/all_to_all | solution.py:439
  65.2 0.0 copy-done.2
  65.2 0.6 slice.20
  66.4 8.5 %collective-permute-start = (f32[1]{0:T(128)}, f32[1]{0:T(128)}, u32[]{:S(2)}, u32[]{:S(2)}) collective-permute-start(f32[1]{0:T(128)} %convert_element_type.3), channel_id=1, source_target_pairs={{0,32},{32,64},{64,96},{1,33},{33,65},{65,97},{2,34},{34,66},{66,9... | collective-permute-start | bytes 20 | tf_op jit(solution)/shard_map/ppermute | solution.py:449
  75.6 0.0 collective-permute-done
  76.2 0.8 all-to-all-done
  77.0 0.1 reduce_sum.19
  77.0 0.6 fusion.1
  77.6 4.9 %collective-permute-start.3 = (f32[1]{0:T(128)}, f32[1]{0:T(128)}, u32[]{:S(2)}, u32[]{:S(2)}) collective-permute-start(f32[1]{0:T(128)} %get-tuple-element.10), channel_id=1, source_target_pairs={{0,32},{32,64},{64,96},{1,33},{33,65},{65,97},{2,34},{34,66},{66,9... | collective-permute-start | bytes 20 | tf_op jit(solution)/shard_map/ppermute | solution.py:449
  82.5 1.3 %collective-permute-start.4 = (f32[1]{0:T(128)}, f32[1]{0:T(128)}, u32[]{:S(2)}, u32[]{:S(2)}) collective-permute-start(f32[1]{0:T(128)} %get-tuple-element.11), channel_id=1, source_target_pairs={{32,0},{64,32},{96,64},{33,1},{65,33},{97,65},{34,2},{66,34},{98,6... | collective-permute-start | bytes 20 | tf_op jit(solution)/shard_map/ppermute | solution.py:449
  83.8 0.0 collective-permute-done.3
  85.1 2.9 %collective-permute-done.4 = f32[1]{0:T(128)} collective-permute-done((f32[1]{0:T(128)}, f32[1]{0:T(128)}, u32[]{:S(2)}, u32[]{:S(2)}) %collective-permute-start.4) | collective-permute-done | bytes 36 | tf_op jit(solution)/shard_map/ppermute | solution.py:449
  89.3 0.6 pad_maximum_fusion.1
  89.8 0.0 collective-permute-done.1
  89.8 0.0 collective-permute-done.2
  89.9 0.0 copy-done
  89.9 0.2 broadcast_select_fusion.1
  90.1 1.2 %pad_maximum_fusion = f32[2,3,4,128,128]{4,3,2,1,0:T(8,128)} fusion(f32[1,3,4,128,128]{4,3,2,1,0:T(8,128)S(1)} %get-tuple-element.7, f32[1,3,4,128,128]{4,3,2,1,0:T(8,128)S(1)} %get-tuple-element.6), kind=kLoop, calls=%fused_computation | loop fusion | flops 393216 | bytes 3145728 | tf_op jit(solution)/shard_map/concatenate | solution.py:482
  (2 shorter events, 0.0 us)
Async XLA Ops:
  51.8 7.7 %copy-start.1 = (f32[2,8,128]{2,1,0:T(8,128)S(1)}, f32[2,8,128]{2,1,0:T(8,128)}, u32[]{:S(2)}) copy-start(f32[2,8,128]{2,1,0:T(8,128)} %get-tuple-element.5) | copy-start | bytes 24580
  51.8 13.4 %copy-start.2 = (s32[2]{0:T(128)S(1)}, s32[2]{0:T(128)}, u32[]{:S(2)}) copy-start(s32[2]{0:T(128)} %bits_ref.1) | copy-start | bytes 28
  51.8 38.1 %copy-start = (f32[2,3,4,128,128]{4,3,2,1,0:T(8,128)S(1)}, f32[2,3,4,128,128]{4,3,2,1,0:T(8,128)}, u32[]{:S(2)}) copy-start(f32[2,3,4,128,128]{4,3,2,1,0:T(8,128)} %get-tuple-element.4) | copy-start | bytes 4718596
  54.6 35.3 %collective-permute-start.1 = (f32[1,3,4,128,128]{4,3,2,1,0:T(8,128)}, f32[1,3,4,128,128]{4,3,2,1,0:T(8,128)S(1)}, u32[]{:S(2)}, u32[]{:S(2)}) collective-permute-start(f32[1,3,4,128,128]{4,3,2,1,0:T(8,128)} %get-tuple-element.8), channel_id=1, source_target_pairs={{0,32},{32,64},{64,96},{1,33},{33,65},{65,97},{2,34},{34,66},{66,9... | collective-permute-start | bytes 2359304 | tf_op jit(solution)/shard_map/ppermute | solution.py:449
  58.2 31.6 %collective-permute-start.2 = (f32[1,3,4,128,128]{4,3,2,1,0:T(8,128)}, f32[1,3,4,128,128]{4,3,2,1,0:T(8,128)S(1)}, u32[]{:S(2)}, u32[]{:S(2)}) collective-permute-start(f32[1,3,4,128,128]{4,3,2,1,0:T(8,128)} %get-tuple-element.9), channel_id=1, source_target_pairs={{32,0},{64,32},{96,64},{33,1},{65,33},{97,65},{34,2},{66,34},{98,6... | collective-permute-start | bytes 2359304 | tf_op jit(solution)/shard_map/ppermute | solution.py:449
  60.2 16.7 %all-to-all-start = ((f32[32,1,2]{2,1,0:T(1,128)}), f32[32,1,2]{2,1,0:T(1,128)S(1)}, u32[]{:S(2)}, u32[]{:S(2)}) async-start(f32[32,1,2]{2,1,0:T(1,128)} %broadcast_in_dim.3), calls=%async_computation | async-start | bytes 32768 | tf_op jit(solution)/shard_map/all_to_all | solution.py:439
  66.4 9.1 %collective-permute-start = (f32[1]{0:T(128)}, f32[1]{0:T(128)}, u32[]{:S(2)}, u32[]{:S(2)}) collective-permute-start(f32[1]{0:T(128)} %convert_element_type.3), channel_id=1, source_target_pairs={{0,32},{32,64},{64,96},{1,33},{33,65},{65,97},{2,34},{34,66},{66,9... | collective-permute-start | bytes 20 | tf_op jit(solution)/shard_map/ppermute | solution.py:449
  77.6 6.2 %collective-permute-start.3 = (f32[1]{0:T(128)}, f32[1]{0:T(128)}, u32[]{:S(2)}, u32[]{:S(2)}) collective-permute-start(f32[1]{0:T(128)} %get-tuple-element.10), channel_id=1, source_target_pairs={{0,32},{32,64},{64,96},{1,33},{33,65},{65,97},{2,34},{34,66},{66,9... | collective-permute-start | bytes 20 | tf_op jit(solution)/shard_map/ppermute | solution.py:449
  82.5 5.5 %collective-permute-start.4 = (f32[1]{0:T(128)}, f32[1]{0:T(128)}, u32[]{:S(2)}, u32[]{:S(2)}) collective-permute-start(f32[1]{0:T(128)} %get-tuple-element.11), channel_id=1, source_target_pairs={{32,0},{64,32},{96,64},{33,1},{65,33},{97,65},{34,2},{66,34},{98,6... | collective-permute-start | bytes 20 | tf_op jit(solution)/shard_map/ppermute | solution.py:449

commit v2 on v1

--- a/solution.py
+++ b/solution.py
@@ -49,7 +49,15 @@
     return 1.0 - 2.0 * sine * sine, 2.0 * sine * cosine
 
 
-def sweep_kernel(
+def far_distances(count):
+    distances, known = [], 2
+    while known < count // 2:
+        distances.append(known)
+        known *= 2
+    return distances
+
+
+def step_kernel(
     spin_hbm,
     bond_hbm,
     level_hbm,
@@ -70,11 +78,31 @@
     bond_z,
     bond_halo,
     trial,
+    meta,
+    meta_got,
+    draws,
+    draws_got,
+    trial_got,
+    share_sum,
+    share_got,
+    total_sum,
+    total_got,
     load_sem,
     bond_send,
     bond_recv,
     send_sem,
     recv_sem,
+    meta_send,
+    meta_recv,
+    draw_send,
+    draw_recv,
+    swap_send,
+    swap_recv,
+    share_send,
+    share_recv,
+    total_send,
+    total_recv,
+    far_sem,
 ):
     planes, rows, columns = spin_in.shape[2:]
     half = rows // 2
@@ -83,7 +111,11 @@
     count = lax.axis_size("gz")
     upper = lax.rem(me + 1, count)
     lower = lax.rem(me + count - 1, count)
+    here_temp = lax.axis_index("temp")
+    temps = lax.axis_size("temp")
     main = pl.ds(PAD, half)
+    got = HALVES + 2
+    distances = far_distances(count)
 
     loads = [
         pltpu.make_async_copy(spin_hbm, spin_in, load_sem.at[0]),
@@ -95,11 +127,18 @@
     for load in loads:
         load.start()
 
+    def temp_towards(slot):
+        return lax.rem(here_temp + 2 * slot - 1 + temps, temps)
+
     barrier = pltpu.get_barrier_semaphore()
     for neighbour in (lower, upper):
         pl.semaphore_signal(
             barrier, inc=1, device_id={"gz": neighbour}, device_id_type=MESH
         )
+    for slot in (0, 1):
+        pl.semaphore_signal(
+            barrier, inc=1, device_id={"temp": temp_towards(slot)}, device_id_type=MESH
+        )
 
     lane = lax.broadcasted_iota(jnp.int32, (half, columns), 1) % 2
     lane_chunk = lax.broadcasted_iota(jnp.int32, (chunk, columns), 1) % 2
@@ -115,6 +154,11 @@
 
     def parity(slot, plane):
         return lax.rem(me * planes + plane + order_of(slot), 2)
+
+    for slot in (0, 1):
+        meta[slot, 0:1] = jnp.full((1, columns), beta_of(slot), jnp.float32)
+        meta[slot, 1:2] = jnp.full((1, columns), order_of(slot), jnp.int32).astype(jnp.float32)
+        meta[slot, 2:3] = jnp.full((1, columns), bits_ref[1], jnp.int32).astype(jnp.float32)
 
     def upward(step, slot):
         return pltpu.make_async_remote_copy(
@@ -144,6 +188,68 @@
         device_id={"gz": upper},
         device_id_type=MESH,
     )
+
+    def along_temp(source, target, send, recv, slot):
+        return pltpu.make_async_remote_copy(
+            src_ref=source,
+            dst_ref=target,
+            send_sem=send,
+            recv_sem=recv,
+            device_id={"temp": temp_towards(slot)},
+            device_id_type=MESH,
+        )
+
+    def meta_copy(slot):
+        return along_temp(
+            meta.at[slot], meta_got.at[1 - slot], meta_send.at[slot], meta_recv.at[1 - slot], slot
+        )
+
+    def draw_copy(slot, plane):
+        return along_temp(
+            draws.at[slot, plane],
+            draws_got.at[1 - slot, plane],
+            draw_send.at[slot, plane],
+            draw_recv.at[1 - slot, plane],
+            slot,
+        )
+
+    def swap_copy(slot, plane):
+        return along_temp(
+            state.at[HALVES, slot, plane, :, main],
+            state.at[got, 1 - slot, plane, :, main],
+            swap_send.at[slot, plane],
+            swap_recv.at[1 - slot, plane],
+            slot,
+        )
+
+    def total_copy(slot):
+        return along_temp(
+            total_sum, total_got.at[1 - slot], total_send.at[slot], total_recv.at[1 - slot], slot
+        )
+
+    def share_copy(distance):
+        return pltpu.make_async_remote_copy(
+            src_ref=share_sum,
+            dst_ref=share_got.at[distance - 1],
+            send_sem=share_send.at[distance - 1],
+            recv_sem=share_recv.at[distance - 1],
+            device_id={"gz": lax.rem(me + distance, count)},
+            device_id_type=MESH,
+        )
+
+    def far_signal(index):
+        if index < len(distances):
+            for move in (distances[index], count - distances[index]):
+                pl.semaphore_signal(
+                    far_sem.at[index],
+                    inc=1,
+                    device_id={"gz": lax.rem(me + move, count)},
+                    device_id_type=MESH,
+                )
+
+    def far_wait(index):
+        if index < len(distances):
+            pl.semaphore_wait(far_sem.at[index], 2)
 
     even_rows = pl.ds(0, half, stride=2)
     odd_rows = pl.ds(1, half, stride=2)
@@ -178,11 +284,13 @@
     lax.fori_loop(0, planes, pack_spins, 0)
     loads[1].wait()
 
-    pl.semaphore_wait(barrier, 2)
+    pl.semaphore_wait(barrier, 4)
     for slot in (0, 1):
         upward(1, slot).start()
         downward(1, slot).start()
     bond_up.start()
+    for slot in (0, 1):
+        meta_copy(slot).start()
 
     def pack_bonds(plane, _):
         even, odd = bond_in[0, plane, even_rows, :], bond_in[0, plane, odd_rows, :]
@@ -218,7 +326,7 @@
             here = pl.ds(start, chunk)
             even_here = pl.ds(2 * start, chunk, stride=2)
             odd_here = pl.ds(2 * start + 1, chunk, stride=2)
-            draws = []
+            packed = []
             for kind in range(3):
                 even = jnp.where(
                     swapped,
@@ -230,9 +338,10 @@
                     heat_in[kind, side, plane, odd_here, :],
                     heat_in[kind, slot, plane, odd_here, :],
                 )
-                draws.append((jnp.where(mask, even, odd), jnp.where(mask, odd, even)))
+                packed.append((jnp.where(mask, even, odd), jnp.where(mask, odd, even)))
+                draws[slot, plane, kind, here] = packed[kind][1]
             for colour in (0, 1):
-                level, height, angle = (draw[colour] for draw in draws)
+                level, height, angle = (draw[colour] for draw in packed)
                 across = jnp.sqrt(jnp.maximum(1.0 - height * height, 0.0))
                 cosine, sine = cos_sin(angle)
                 trial[slot, colour, plane, 0, here] = level
@@ -240,11 +349,19 @@
                 trial[slot, colour, plane, 2, here] = across * sine
                 trial[slot, colour, plane, 3, here] = height
 
-    def pulls(step, slot, plane, pattern, mask, start):
+    def bonds_of(pattern, plane, start):
         here = pl.ds(start, chunk)
-        east, west = bond_x[pattern, plane - 1, 0, here], bond_x[pattern, plane - 1, 1, here]
-        near, far = bond_ys[plane - 1, here], bond_yo[pattern, plane - 1, here]
-        above, below = bond_z[pattern, plane, here], bond_z[pattern, plane - 1, here]
+        return (
+            bond_x[pattern, plane - 1, 0, here],
+            bond_x[pattern, plane - 1, 1, here],
+            bond_ys[plane - 1, here],
+            bond_yo[pattern, plane - 1, here],
+            bond_z[pattern, plane, here],
+            bond_z[pattern, plane - 1, here],
+        )
+
+    def pulls(step, slot, plane, bonds, mask, start):
+        east, west, near, far, above, below = bonds
         at = pl.ds(PAD + start, chunk)
         out = []
         for part in range(3):
@@ -269,12 +386,24 @@
         mask = lane_chunk == pattern
         for start in range(0, half, chunk):
             at = pl.ds(PAD + start, chunk)
-            pulled = pulls(step, slot, plane, pattern, mask, start)
+            pulled = pulls(step, slot, plane, bonds_of(pattern, plane, start), mask, start)
             old = [state[step - 1, slot, plane, part, at] for part in range(3)]
             scale = 2.0 * dot(old, pulled) / jnp.maximum(dot(pulled, pulled), 0.01)
             for part in range(3):
                 state[step + 1, slot, plane, part, at] = scale * pulled[part] - old[part]
         wrap_rows(step + 1, slot, plane)
+
+    def heated(pulled, beta, level, draw):
+        square = jnp.maximum(dot(pulled, pulled), 0.01)
+        inverse = lax.rsqrt(square)
+        reach = beta * (square * inverse)
+        axis = [part * inverse for part in pulled]
+        cosine = 1.0 + jnp.log((1.0 - level) + level * jnp.exp(-2.0 * reach)) / reach
+        along = dot(draw, axis)
+        tangent = [draw[part] - along * axis[part] for part in range(3)]
+        norm = lax.rsqrt(jnp.maximum(dot(tangent, tangent), 0.0001))
+        side = jnp.sqrt(jnp.maximum(1.0 - cosine * cosine, 0.0)) * norm
+        return [cosine * axis[part] + side * tangent[part] for part in range(3)]
 
     def heat_plane(step, slot, plane):
         colour = step - OR_HALVES - 1
@@ -285,51 +414,44 @@
         for start in range(0, half, chunk):
             at = pl.ds(PAD + start, chunk)
             here = pl.ds(start, chunk)
-            pulled = pulls(step, slot, plane, pattern, mask, start)
-            square = jnp.maximum(dot(pulled, pulled), 0.01)
-            inverse = lax.rsqrt(square)
-            reach = beta * (square * inverse)
-            axis = [part * inverse for part in pulled]
+            pulled = pulls(step, slot, plane, bonds_of(pattern, plane, start), mask, start)
             level = trial[slot, colour, plane - 1, 0, here]
-            cosine = 1.0 + jnp.log((1.0 - level) + level * jnp.exp(-2.0 * reach)) / reach
             draw = [trial[slot, colour, plane - 1, part, here] for part in (1, 2, 3)]
-            along = dot(draw, axis)
-            tangent = [draw[part] - along * axis[part] for part in range(3)]
-            norm = lax.rsqrt(jnp.maximum(dot(tangent, tangent), 0.0001))
-            side = jnp.sqrt(jnp.maximum(1.0 - cosine * cosine, 0.0)) * norm
-            fresh = [cosine * axis[part] + side * tangent[part] for part in range(3)]
+            fresh = heated(pulled, beta, level, draw)
             for part in range(3):
                 state[step + 1, slot, plane, part, at] = fresh[part]
             gain = gain + jnp.sum(dot(fresh, pulled).reshape(-1, 8, columns), axis=0)
         wrap_rows(step + 1, slot, plane)
         return gain
 
-    def boundary_first(index):
-        return jnp.where(index == 0, 1, jnp.where(index == 1, planes, index))
-
-    def halves(step, slot, body, send, initial):
+    def halves(step, slot, body, initial, send=True, swap=False):
         def visit(index, carry):
-            plane = boundary_first(index)
-
-            @pl.when(index == 0)
+            outer = index < 2
+            low = outer & (lax.rem(index + me, 2) == 0)
+            high = outer & (lax.rem(index + me, 2) == 1)
+            plane = jnp.where(low, 1, jnp.where(high, planes, index))
+
+            @pl.when(low)
             def _():
                 upward(step, slot).wait_recv()
 
-            @pl.when(index == 1)
+            @pl.when(high)
             def _():
                 downward(step, slot).wait_recv()
 
             carry = body(step, slot, plane, carry)
             if send:
 
-                @pl.when(index == 0)
+                @pl.when(low)
                 def _():
                     downward(step + 1, slot).start()
 
-                @pl.when(index == 1)
+                @pl.when(high)
                 def _():
                     upward(step + 1, slot).start()
 
+            if swap:
+                swap_copy(slot, plane).start()
             return carry
 
         return lax.fori_loop(0, planes, visit, initial)
@@ -341,112 +463,183 @@
     def heat_body(step, slot, plane, carry):
         return carry + heat_plane(step, slot, plane)
 
+    share = planes // OR_HALVES
+
     def relax_round(visit, _):
         step = visit // 2 + 1
         slot = lax.rem(visit, 2)
-        halves(step, slot, relax_body, True, 0)
-        share = planes // OR_HALVES
+        halves(step, slot, relax_body, 0)
 
         def fill(index, _):
-            pack_heat_dynamic(slot, (step - 1) * share + index)
+            plane = (step - 1) * share + index
+            pack_heat(slot, plane)
+            draw_copy(slot, plane).start()
             return 0
 
         lax.fori_loop(0, share, fill, 0)
-        return 0
-
-    def pack_heat_dynamic(slot, plane):
-        pack_heat(slot, plane)
+
+        @pl.when(visit == 1)
+        def _():
+            far_signal(0)
+
+        return 0
 
     lax.fori_loop(0, 2 * OR_HALVES, relax_round, 0)
-
-    for step in (OR_HALVES + 1, OR_HALVES + 2):
-        last = step == OR_HALVES + 2
-
-        def heat_round(slot, _, step=step, last=last):
-            zero = jnp.zeros((8, columns), jnp.float32)
-            gain = halves(step, slot, heat_body, not last, zero)
-            if last:
-                energy_ref[slot] = gain
+    far_wait(0)
+    far_signal(1)
+
+    zero = jnp.zeros((8, columns), jnp.float32)
+
+    def first_heat(slot, _):
+        halves(OR_HALVES + 1, slot, heat_body, zero, swap=True)
+        return 0
+
+    lax.fori_loop(0, 2, first_heat, 0)
+    far_wait(1)
+    far_signal(2)
+
+    def second_heat(slot, _):
+        gain = halves(OR_HALVES + 2, slot, heat_body, zero, send=False)
+        share_sum[pl.ds(slot, 1), :] = jnp.sum(gain, axis=0, keepdims=True)
+        return 0
+
+    lax.fori_loop(0, 2, second_heat, 0)
+    far_wait(2)
+
+    def give_share(distance, _):
+        share_copy(distance).start()
+        return 0
+
+    lax.fori_loop(1, count, give_share, 0)
+
+    def pass_on(slot, _):
+        swap_copy(1 - slot, 1).wait_recv()
+        downward(got, slot).start()
+        swap_copy(1 - slot, planes).wait_recv()
+        upward(got, slot).start()
+        return 0
+
+    lax.fori_loop(0, 2, pass_on, 0)
+
+    def prepare(visit, _):
+        slot = visit // planes
+        plane = lax.rem(visit, planes)
+        draw_copy(1 - slot, plane).wait_recv()
+        for start in range(0, half, chunk):
+            here = pl.ds(start, chunk)
+            level, height, angle = (draws_got[slot, plane, kind, here] for kind in range(3))
+            across = jnp.sqrt(jnp.maximum(1.0 - height * height, 0.0))
+            cosine, sine = cos_sin(angle)
+            trial_got[slot, plane, 0, here] = level
+            trial_got[slot, plane, 1, here] = across * cosine
+            trial_got[slot, plane, 2, here] = across * sine
+            trial_got[slot, plane, 3, here] = height
+        return 0
+
+    lax.fori_loop(0, 2 * planes, prepare, 0)
+
+    def take_share(distance, sums):
+        share_copy(distance).wait_recv()
+        return sums + share_got[distance - 1]
+
+    total_sum[...] = lax.fori_loop(1, count, take_share, share_sum[...])
+    for slot in (0, 1):
+        total_copy(slot).start()
+        meta_copy(1 - slot).wait_recv()
+
+    taking = [
+        (meta_got[0, 2:3] > 0.5) & (here_temp > 0),
+        jnp.full((1, columns), bits_ref[1], jnp.int32) * jnp.where(here_temp < temps - 1, 1, 0) > 0,
+    ]
+
+    def finish_plane(slot, plane):
+        take = jnp.broadcast_to(taking[slot], (chunk, columns))
+        flip = jnp.broadcast_to(meta_got[slot, 1:2] > 0.5, (chunk, columns))
+        beta = meta_got[slot, 0:1]
+        base = lax.rem(me * planes + plane - 1, 2)
+        first_mask = (lane_chunk == base) ^ flip
+        own_mask = lane_chunk == parity(slot, plane - 1)
+        unpack_mask = jnp.where(take, first_mask.astype(jnp.int32), own_mask.astype(jnp.int32)) > 0
+        for start in range(0, half, chunk):
+            at = pl.ds(PAD + start, chunk)
+            here = pl.ds(start, chunk)
+            plain = bonds_of(1 - base, plane, start)
+            other = bonds_of(base, plane, start)
+            bonds = [jnp.where(flip, b, a) for a, b in zip(plain, other)]
+            pulled = pulls(got, slot, plane, bonds, ~first_mask, start)
+            level = trial_got[slot, plane - 1, 0, here]
+            draw = [trial_got[slot, plane - 1, part, here] for part in (1, 2, 3)]
+            fresh = heated(pulled, beta, level, draw)
+            for part in range(3):
+                first = jnp.where(
+                    take, state[got, slot, plane, part, at], state[HALVES, slot, plane, part, at]
+                )
+                second = jnp.where(take, fresh[part], state[HALVES + 1, slot, plane, part, at])
+                out_ref[slot, part, plane - 1, pl.ds(2 * start, chunk, stride=2), :] = jnp.where(
+                    unpack_mask, first, second
+                )
+                out_ref[slot, part, plane - 1, pl.ds(2 * start + 1, chunk, stride=2), :] = jnp.where(
+                    unpack_mask, second, first
+                )
+
+    for slot in (0, 1):
+
+        def arrive(plane, _, slot=slot):
+            @pl.when((plane > 1) & (plane < planes))
+            def _():
+                swap_copy(1 - slot, plane).wait_recv()
+
+            wrap_rows(got, slot, plane)
             return 0
 
-        lax.fori_loop(0, 2, heat_round, 0)
-
-    def unpack(plane, _):
-        for slot in (0, 1):
-            mask = lane == parity(slot, plane)
-            for part in range(3):
-                first = state[HALVES, slot, plane + 1, part, main]
-                second = state[HALVES + 1, slot, plane + 1, part, main]
-                out_ref[slot, part, plane, even_rows, :] = jnp.where(mask, first, second)
-                out_ref[slot, part, plane, odd_rows, :] = jnp.where(mask, second, first)
-        return 0
-
-    lax.fori_loop(0, planes, unpack, 0)
+        def inner(plane, _, slot=slot):
+            finish_plane(slot, plane)
+            return 0
+
+        lax.fori_loop(1, planes + 1, arrive, 0)
+        upward(got, slot).wait_recv()
+        downward(got, slot).wait_recv()
+        lax.fori_loop(1, planes + 1, inner, 0)
+
+    for slot in (0, 1):
+        total_copy(1 - slot).wait_recv()
+        own = total_sum[slot : slot + 1]
+        other = total_got[slot, 1 - slot : 2 - slot]
+        value = jnp.where(taking[slot], other, own)
+        sites = float(columns * rows * planes * count)
+        energy_ref[slot] = -jnp.sum(value) / sites
 
     bond_up.wait_send()
-
-    def drain(index, _):
+    for slot in (0, 1):
+        meta_copy(slot).wait_send()
+        total_copy(slot).wait_send()
+
+    def drain_halo(index, _):
         step = index // 2 + 1
         slot = lax.rem(index, 2)
         upward(step, slot).wait_send()
         downward(step, slot).wait_send()
         return 0
 
-    lax.fori_loop(0, 2 * HALVES, drain, 0)
-
-
-def sweep(spin_state, couplings, level, height, angle, beta, order, bits):
-    slots, parts, planes, rows, columns = spin_state.shape
-    half = rows // 2
-    f32 = jnp.float32
-    any_space = pl.BlockSpec(memory_space=pl.ANY)
-    smem = pl.BlockSpec(memory_space=pltpu.SMEM)
-    vmem = pl.BlockSpec(memory_space=pltpu.VMEM)
-    return pl.pallas_call(
-        sweep_kernel,
-        out_shape=(
-            jax.ShapeDtypeStruct(spin_state.shape, f32),
-            jax.ShapeDtypeStruct((slots, 8, columns), f32),
-        ),
-        in_specs=[any_space] * 5 + [smem] * 3,
-        out_specs=(vmem, vmem),
-        scratch_shapes=[
-            pltpu.VMEM(spin_state.shape, f32),
-            pltpu.VMEM(couplings.shape, f32),
-            pltpu.VMEM((3,) + level.shape, f32),
-            pltpu.VMEM((HALVES + 2, slots, planes + 2, 3, half + 2 * PAD, columns), f32),
-            pltpu.VMEM((2, planes, 2, half, columns), f32),
-            pltpu.VMEM((2, planes, half, columns), f32),
-            pltpu.VMEM((planes, half, columns), f32),
-            pltpu.VMEM((2, planes + 1, half, columns), f32),
-            pltpu.VMEM((rows, columns), f32),
-            pltpu.VMEM((slots, 2, planes, 4, half, columns), f32),
-            pltpu.SemaphoreType.DMA((5,)),
-            pltpu.SemaphoreType.DMA,
-            pltpu.SemaphoreType.DMA,
-            pltpu.SemaphoreType.DMA((HALVES + 1, slots, 2)),
-            pltpu.SemaphoreType.DMA((HALVES + 1, slots, 2)),
-        ],
-        compiler_params=pltpu.CompilerParams(
-            collective_id=0, has_side_effects=True, vmem_limit_bytes=56 * 1024 * 1024
-        ),
-        name="sweep",
-    )(spin_state, couplings, level, height, angle, beta, order, bits)
-
-
-def copy_for_each(array, axis):
-    copies = jnp.broadcast_to(array, (lax.axis_size(axis), *array.shape))
-    return lax.all_to_all(copies, axis, split_axis=0, concat_axis=0, tiled=True)
-
-
-def of_everyone(array, axis):
-    return jnp.sum(copy_for_each(array, axis), axis=0)
-
-
-def shifted(block, axis, distance):
-    devices = range(lax.axis_size(axis))
-    route = [(i - distance, i) for i in devices if i - distance in devices]
-    return lax.ppermute(block, axis, route)
+    lax.fori_loop(0, 2 * HALVES, drain_halo, 0)
+    for slot in (0, 1):
+        upward(got, slot).wait_send()
+        downward(got, slot).wait_send()
+
+    def drain_temp(index, _):
+        slot = index // planes
+        plane = lax.rem(index, planes)
+        draw_copy(slot, plane).wait_send()
+        swap_copy(slot, plane + 1).wait_send()
+        return 0
+
+    lax.fori_loop(0, 2 * planes, drain_temp, 0)
+
+    def drain_share(distance, _):
+        share_copy(distance).wait_send()
+        return 0
+
+    lax.fori_loop(1, count, drain_share, 0)
 
 
 def on_device(
@@ -459,8 +652,65 @@
     heat_angle,
     swap_bits,
 ):
-    planes, rows, columns = spin_state.shape[2:]
-    spin_now, gains = sweep(
+    slots, parts, planes, rows, columns = spin_state.shape
+    half = rows // 2
+    count = lax.axis_size("gz")
+    f32 = jnp.float32
+    dma = pltpu.SemaphoreType.DMA
+    any_space = pl.BlockSpec(memory_space=pl.ANY)
+    smem = pl.BlockSpec(memory_space=pltpu.SMEM)
+    vmem = pl.BlockSpec(memory_space=pltpu.VMEM)
+    steps = HALVES + 3
+    return pl.pallas_call(
+        step_kernel,
+        out_shape=(
+            jax.ShapeDtypeStruct(spin_state.shape, f32),
+            jax.ShapeDtypeStruct((slots,), f32),
+        ),
+        in_specs=[any_space] * 5 + [smem] * 3,
+        out_specs=(vmem, smem),
+        scratch_shapes=[
+            pltpu.VMEM(spin_state.shape, f32),
+            pltpu.VMEM(couplings.shape, f32),
+            pltpu.VMEM((3,) + heat_level.shape, f32),
+            pltpu.VMEM((steps, slots, planes + 2, 3, half + 2 * PAD, columns), f32),
+            pltpu.VMEM((2, planes, 2, half, columns), f32),
+            pltpu.VMEM((2, planes, half, columns), f32),
+            pltpu.VMEM((planes, half, columns), f32),
+            pltpu.VMEM((2, planes + 1, half, columns), f32),
+            pltpu.VMEM((rows, columns), f32),
+            pltpu.VMEM((slots, 2, planes, 4, half, columns), f32),
+            pltpu.VMEM((slots, 8, columns), f32),
+            pltpu.VMEM((slots, 8, columns), f32),
+            pltpu.VMEM((slots, planes, 3, half, columns), f32),
+            pltpu.VMEM((slots, planes, 3, half, columns), f32),
+            pltpu.VMEM((slots, planes, 4, half, columns), f32),
+            pltpu.VMEM((2, columns), f32),
+            pltpu.VMEM((count - 1, 2, columns), f32),
+            pltpu.VMEM((2, columns), f32),
+            pltpu.VMEM((slots, 2, columns), f32),
+            dma((5,)),
+            dma,
+            dma,
+            dma((steps, slots, 2)),
+            dma((steps, slots, 2)),
+            dma((slots,)),
+            dma((slots,)),
+            dma((slots, planes)),
+            dma((slots, planes)),
+            dma((slots, planes + 1)),
+            dma((slots, planes + 1)),
+            dma((count - 1,)),
+            dma((count - 1,)),
+            dma((slots,)),
+            dma((slots,)),
+            pltpu.SemaphoreType.REGULAR((max(1, len(far_distances(count))),)),
+        ],
+        compiler_params=pltpu.CompilerParams(
+            collective_id=0, has_side_effects=True, vmem_limit_bytes=56 * 1024 * 1024
+        ),
+        name="replica_step",
+    )(
         spin_state,
         couplings,
         heat_level,
@@ -470,28 +720,6 @@
         colour_order,
         swap_bits,
     )
-    total_sites = float(columns * rows * planes * lax.axis_size("gz"))
-    energy_now = of_everyone(-jnp.sum(gains, axis=(1, 2)), "gz") / total_sites
-    below_spin, below_energy, below_bit = shifted(
-        (spin_now[1:], energy_now[1:], swap_bits[1:].astype(jnp.float32)), "temp", 1
-    )
-    above_spin, above_energy = shifted((spin_now[:1], energy_now[:1]), "temp", -1)
-    top_device = lax.axis_index("temp") == lax.axis_size("temp") - 1
-    take_below = below_bit[0] > 0.5
-    take_above = (swap_bits[1] != 0) & ~top_device
-    spin_final = jnp.concatenate(
-        [
-            jnp.where(take_below, below_spin, spin_now[:1]),
-            jnp.where(take_above, above_spin, spin_now[1:]),
-        ]
-    )
-    energies = jnp.concatenate(
-        [
-            jnp.where(take_below, below_energy, energy_now[:1]),
-            jnp.where(take_above, above_energy, energy_now[1:]),
-        ]
-    )
-    return (spin_final, energies)
 
 
 def solution(mesh):

time: 91.6 us -> 68.1 us (0.74)
  starting transfers between devices: 24.5 us -> 0 us
  Pallas kernels: 51.1 us -> 64.1 us
  between operations: 5.24 us -> 0.65 us
  waiting for transfers between devices: 3.66 us -> 0 us
  other arithmetic: 2.19 us -> 0 us
  local copies, waits for them, and re-layouts: 4.59 us -> 3.22 us
    ppermute x5 -> x0, starting transfers between devices: 19.6 us -> none  [shifted(): return lax.ppermute(block, axis, route)]
    pallas_call x1, Pallas kernels: 51.1 us -> 64.1 us  [on_device(): pl.pallas_call(step_kernel, out_shape=(jax.ShapeDtypeStruct(spin_state.sh...]
    all_to_all x1 -> x0, starting transfers between devices: 4.94 us -> none  [copy_for_each(): return lax.all_to_all(copies, axis, split_axis=0, concat_axis=0, tiled=True)]
    slice x3 -> x0, local copies, waits for them, and re-layouts: 3.96 us -> none  [the longest x1 2.78 us: on_device(): spin_now[1:]]
    unnamed x6 -> x4, local copies, waits for them, and re-layouts: 0.01 us -> 3.22 us
    ppermute x5 -> x0, waiting for transfers between devices: 2.88 us -> none  [shifted(): return lax.ppermute(block, axis, route)]
    concatenate x2 -> x0, other arithmetic: 1.83 us -> none  [the longest x1 1.25 us: on_device(): jnp.concatenate([jnp.where(take_below, below_spin, spin_now[:1]), jnp.whe...]
  transfers between devices with their start and end apart: 6 -> 0, of which waited for: 2 -> 0; matrix products, arithmetic and copies ran while one was open for 3% -> 0% of each run, Pallas kernels for 0% -> 0%
where the time goes in v2:
time: 68.1 us; the launch traced here: 68 us
  Pallas kernels  64.1 us (94%)
  local copies, waits for them, and re-layouts  3.22 us (5%)
    pallas_call x1, Pallas kernels, on_device(): pl.pallas_call(step_kernel, out_shape=(jax.ShapeDtypeStruct(spin_state.sh...  64.1 us
    unnamed x4, local copies, waits for them, and re-layouts  3.22 us

profile of v2, /device:TPU:40, one launch (start us, length us, event | category | flops | bytes accessed | tf_op | source)
XLA Modules:
  0.0 68.0 jit_solution(14108005189084816750)
XLA Ops:
  0.6 64.1 %replica_step.1 = (f32[2,3,4,128,128]{4,3,2,1,0:T(8,128)}, f32[2]{0:T(128)}) custom-call(f32[2,3,4,128,128]{4,3,2,1,0:T(8,128)} %spin_hbm.1, f32[3,4,128,128]{3,2,1,0:T(8,128)} %bond_hbm.1, f32[2,4,128,128]{3,2,1,0:T(8,128)} %level_hbm.1, f32[2,4,128,128]{3,2,1,0:T(8,128)} %height_hbm.1, f32[2,4,128,128]{3,2,1,0:T(8,128)} %angle_hbm.1, f32[2]{0:T(128)} %beta_ref.1, ...), custom_call_target="tpu_custom_call" | custom-call | tf_op jit(solution)/shard_map/replica_step/pallas_call | solution.py:664
  64.7 0.0 copy-start
  64.7 2.7 %copy.12 = f32[2,3,4,128,128]{4,3,2,1,0:T(8,128)} copy(f32[2,3,4,128,128]{4,3,2,1,0:T(8,128)} %get-tuple-element.4) | data formatting | bytes 3145728
  67.4 0.0 copy-done
  67.5 0.5 copy.13
Async XLA Ops:
  64.7 2.7 %copy-start = (f32[2]{0:T(128)S(1)}, f32[2]{0:T(128)}, u32[]{:S(2)}) copy-start(f32[2]{0:T(128)} %get-tuple-element.5) | copy-start | bytes 28

commit v3 on v2

--- a/solution.py
+++ b/solution.py
@@ -11,6 +11,7 @@
 OR_HALVES = 2 * OR_SWEEPS
 HALVES = OR_HALVES + 2
 PAD = 8
+CHUNKS = 4
 MESH = pl.DeviceIdType.MESH
 
 SIN_TERMS = (
@@ -63,11 +64,14 @@
     level_hbm,
     height_hbm,
     angle_hbm,
+    beta_hbm,
+    order_hbm,
+    bits_hbm,
+    out_ref,
+    energy_ref,
     beta_ref,
     order_ref,
     bits_ref,
-    out_ref,
-    energy_ref,
     spin_in,
     bond_in,
     heat_in,
@@ -87,6 +91,9 @@
     share_got,
     total_sum,
     total_got,
+    gains,
+    small_sem,
+    spin_sem,
     load_sem,
     bond_send,
     bond_recv,
@@ -106,7 +113,8 @@
 ):
     planes, rows, columns = spin_in.shape[2:]
     half = rows // 2
-    chunk = min(16, half)
+    piece = half // CHUNKS
+    chunk = min(16, piece)
     me = lax.axis_index("gz")
     count = lax.axis_size("gz")
     upper = lax.rem(me + 1, count)
@@ -117,13 +125,33 @@
     got = HALVES + 2
     distances = far_distances(count)
 
+    far_low = lax.rem(me, 2) == 0
+    far_plane = jnp.where(far_low, 1, planes)
+    near_plane = jnp.where(far_low, planes, 1)
+
+    small = [
+        pltpu.make_async_copy(source, target, small_sem.at[index])
+        for index, (source, target) in enumerate(
+            ((bits_hbm, bits_ref), (order_hbm, order_ref), (beta_hbm, beta_ref))
+        )
+    ]
+
+    def spin_load(plane):
+        return pltpu.make_async_copy(
+            spin_hbm.at[:, :, plane - 1], spin_in.at[:, :, plane - 1], spin_sem.at[plane - 1]
+        )
+
     loads = [
-        pltpu.make_async_copy(spin_hbm, spin_in, load_sem.at[0]),
-        pltpu.make_async_copy(bond_hbm, bond_in, load_sem.at[1]),
-        pltpu.make_async_copy(level_hbm, heat_in.at[0], load_sem.at[2]),
-        pltpu.make_async_copy(height_hbm, heat_in.at[1], load_sem.at[3]),
-        pltpu.make_async_copy(angle_hbm, heat_in.at[2], load_sem.at[4]),
+        pltpu.make_async_copy(bond_hbm, bond_in, load_sem.at[0]),
+        pltpu.make_async_copy(level_hbm, heat_in.at[0], load_sem.at[1]),
+        pltpu.make_async_copy(height_hbm, heat_in.at[1], load_sem.at[2]),
+        pltpu.make_async_copy(angle_hbm, heat_in.at[2], load_sem.at[3]),
     ]
+    for load in small:
+        load.start()
+    plane_order = [far_plane, near_plane] + list(range(2, planes))
+    for plane in plane_order:
+        spin_load(plane).start()
     for load in loads:
         load.start()
 
@@ -142,6 +170,8 @@
 
     lane = lax.broadcasted_iota(jnp.int32, (half, columns), 1) % 2
     lane_chunk = lax.broadcasted_iota(jnp.int32, (chunk, columns), 1) % 2
+    for load in small:
+        load.wait()
     swapped = bits_ref[0] != 0
 
     def order_of(slot):
@@ -160,28 +190,30 @@
         meta[slot, 1:2] = jnp.full((1, columns), order_of(slot), jnp.int32).astype(jnp.float32)
         meta[slot, 2:3] = jnp.full((1, columns), bits_ref[1], jnp.int32).astype(jnp.float32)
 
-    def upward(step, slot):
+    def halo(step, slot, down, rows_at, part):
         return pltpu.make_async_remote_copy(
-            src_ref=state.at[step, slot, planes, :, main],
-            dst_ref=state.at[step, slot, 0, :, main],
-            send_sem=send_sem.at[step, slot, 0],
-            recv_sem=recv_sem.at[step, slot, 0],
-            device_id={"gz": upper},
+            src_ref=state.at[step, slot, jnp.where(down, 1, planes), :, rows_at],
+            dst_ref=state.at[step, slot, jnp.where(down, planes + 1, 0), :, rows_at],
+            send_sem=send_sem.at[slot, part],
+            recv_sem=recv_sem.at[1 if step is got else lax.rem(step, 2), slot, part],
+            device_id={"gz": jnp.where(down, lower, upper)},
             device_id_type=MESH,
         )
 
-    def downward(step, slot):
-        return pltpu.make_async_remote_copy(
-            src_ref=state.at[step, slot, 1, :, main],
-            dst_ref=state.at[step, slot, planes + 1, :, main],
-            send_sem=send_sem.at[step, slot, 1],
-            recv_sem=recv_sem.at[step, slot, 1],
-            device_id={"gz": lower},
-            device_id_type=MESH,
-        )
+    def far_out(step, slot, part):
+        return halo(step, slot, far_low, pl.ds(PAD + part * piece, piece), part)
+
+    def far_in(step, slot, part):
+        return halo(step, slot, ~far_low, pl.ds(PAD + part * piece, piece), part)
+
+    def near_out(step, slot):
+        return halo(step, slot, ~far_low, main, CHUNKS)
+
+    def near_in(step, slot):
+        return halo(step, slot, far_low, main, CHUNKS)
 
     bond_up = pltpu.make_async_remote_copy(
-        src_ref=bond_in.at[2, planes - 1],
+        src_ref=bond_hbm.at[2, planes - 1],
         dst_ref=bond_halo,
         send_sem=bond_send,
         recv_sem=bond_recv,
@@ -208,17 +240,22 @@
         return along_temp(
             draws.at[slot, plane],
             draws_got.at[1 - slot, plane],
-            draw_send.at[slot, plane],
-            draw_recv.at[1 - slot, plane],
+            draw_send,
+            draw_recv.at[1 - slot],
             slot,
+        )
+
+    def all_draws(slot):
+        return along_temp(
+            draws.at[slot], draws_got.at[1 - slot], draw_send, draw_recv.at[1 - slot], slot
         )
 
     def swap_copy(slot, plane):
         return along_temp(
             state.at[HALVES, slot, plane, :, main],
             state.at[got, 1 - slot, plane, :, main],
-            swap_send.at[slot, plane],
-            swap_recv.at[1 - slot, plane],
+            swap_send.at[slot, plane - 1],
+            swap_recv.at[1 - slot, plane - 1],
             slot,
         )
 
@@ -231,11 +268,20 @@
         return pltpu.make_async_remote_copy(
             src_ref=share_sum,
             dst_ref=share_got.at[distance - 1],
-            send_sem=share_send.at[distance - 1],
-            recv_sem=share_recv.at[distance - 1],
+            send_sem=share_send,
+            recv_sem=share_recv,
             device_id={"gz": lax.rem(me + distance, count)},
             device_id_type=MESH,
         )
+
+    all_shares = pltpu.make_async_remote_copy(
+        src_ref=share_got,
+        dst_ref=share_got,
+        send_sem=share_send,
+        recv_sem=share_recv,
+        device_id={"gz": upper},
+        device_id_type=MESH,
+    )
 
     def far_signal(index):
         if index < len(distances):
@@ -263,34 +309,44 @@
                 step, slot, plane, part, PAD : PAD + 1
             ]
 
-    def pack_spins(plane, _):
+    def pack_spins(plane):
         for part in range(3):
             pairs = [
-                (spin_in[r, part, plane, even_rows, :], spin_in[r, part, plane, odd_rows, :])
+                (
+                    spin_in[r, part, plane - 1, even_rows, :],
+                    spin_in[r, part, plane - 1, odd_rows, :],
+                )
                 for r in (0, 1)
             ]
             for slot in (0, 1):
                 even = jnp.where(swapped, pairs[1 - slot][0], pairs[slot][0])
                 odd = jnp.where(swapped, pairs[1 - slot][1], pairs[slot][1])
-                mask = lane == parity(slot, plane)
-                state[0, slot, plane + 1, part, main] = jnp.where(mask, even, odd)
-                state[1, slot, plane + 1, part, main] = jnp.where(mask, odd, even)
+                mask = lane == parity(slot, plane - 1)
+                state[0, slot, plane, part, main] = jnp.where(mask, even, odd)
+                state[1, slot, plane, part, main] = jnp.where(mask, odd, even)
         for slot in (0, 1):
-            wrap_rows(1, slot, plane + 1)
-            wrap_rows(0, slot, plane + 1)
-        return 0
-
+            wrap_rows(1, slot, plane)
+
+    pl.semaphore_wait(barrier, 4)
+    bond_up.start()
+    spin_load(far_plane).wait()
+    pack_spins(far_plane)
+    for slot in (0, 1):
+        for part in range(CHUNKS):
+            far_out(1, slot, part).start()
+    spin_load(near_plane).wait()
+    pack_spins(near_plane)
+    for slot in (0, 1):
+        near_out(1, slot).start()
+        meta_copy(slot).start()
+
+    def pack_inner(plane, _):
+        spin_load(plane).wait()
+        pack_spins(plane)
+        return 0
+
+    lax.fori_loop(2, planes, pack_inner, 0)
     loads[0].wait()
-    lax.fori_loop(0, planes, pack_spins, 0)
-    loads[1].wait()
-
-    pl.semaphore_wait(barrier, 4)
-    for slot in (0, 1):
-        upward(1, slot).start()
-        downward(1, slot).start()
-    bond_up.start()
-    for slot in (0, 1):
-        meta_copy(slot).start()
 
     def pack_bonds(plane, _):
         even, odd = bond_in[0, plane, even_rows, :], bond_in[0, plane, odd_rows, :]
@@ -311,13 +367,6 @@
         return 0
 
     lax.fori_loop(0, planes, pack_bonds, 0)
-    bond_up.wait_recv()
-    even, odd = bond_halo[even_rows, :], bond_halo[odd_rows, :]
-    bond_z[0, 0] = jnp.where(lane == 0, even, odd)
-    bond_z[1, 0] = jnp.where(lane == 0, odd, even)
-
-    for load in loads[2:]:
-        load.wait()
 
     def pack_heat(slot, plane):
         side = 1 - slot
@@ -381,17 +430,19 @@
     def dot(first, second):
         return first[0] * second[0] + first[1] * second[1] + first[2] * second[2]
 
-    def relax_plane(step, slot, plane):
-        pattern = lax.rem(parity(slot, plane - 1) + step + 1, 2)
-        mask = lane_chunk == pattern
-        for start in range(0, half, chunk):
-            at = pl.ds(PAD + start, chunk)
-            pulled = pulls(step, slot, plane, bonds_of(pattern, plane, start), mask, start)
-            old = [state[step - 1, slot, plane, part, at] for part in range(3)]
-            scale = 2.0 * dot(old, pulled) / jnp.maximum(dot(pulled, pulled), 0.01)
-            for part in range(3):
-                state[step + 1, slot, plane, part, at] = scale * pulled[part] - old[part]
-        wrap_rows(step + 1, slot, plane)
+    def colour_of(step, slot, plane):
+        return lax.rem(parity(slot, plane - 1) + step + 1, 2)
+
+    def relax_rows(step, slot, plane, start):
+        pattern = colour_of(step, slot, plane)
+        at = pl.ds(PAD + start, chunk)
+        bonds = bonds_of(pattern, plane, start)
+        pulled = pulls(step, slot, plane, bonds, lane_chunk == pattern, start)
+        old = [state[step - 1, slot, plane, part, at] for part in range(3)]
+        scale = 2.0 * dot(old, pulled) / jnp.maximum(dot(pulled, pulled), 0.01)
+        for part in range(3):
+            state[step + 1, slot, plane, part, at] = scale * pulled[part] - old[part]
+        return 0
 
     def heated(pulled, beta, level, draw):
         square = jnp.maximum(dot(pulled, pulled), 0.01)
@@ -405,78 +456,84 @@
         side = jnp.sqrt(jnp.maximum(1.0 - cosine * cosine, 0.0)) * norm
         return [cosine * axis[part] + side * tangent[part] for part in range(3)]
 
-    def heat_plane(step, slot, plane):
+    def heat_rows(step, slot, plane, start):
         colour = step - OR_HALVES - 1
-        pattern = lax.rem(parity(slot, plane - 1) + step + 1, 2)
-        mask = lane_chunk == pattern
-        beta = beta_of(slot)
-        gain = jnp.zeros((8, columns), jnp.float32)
+        pattern = colour_of(step, slot, plane)
+        at = pl.ds(PAD + start, chunk)
+        here = pl.ds(start, chunk)
+        bonds = bonds_of(pattern, plane, start)
+        pulled = pulls(step, slot, plane, bonds, lane_chunk == pattern, start)
+        level = trial[slot, colour, plane - 1, 0, here]
+        draw = [trial[slot, colour, plane - 1, part, here] for part in (1, 2, 3)]
+        fresh = heated(pulled, beta_of(slot), level, draw)
+        for part in range(3):
+            state[step + 1, slot, plane, part, at] = fresh[part]
+        return jnp.sum(dot(fresh, pulled).reshape(-1, 8, columns), axis=0)
+
+    def whole_plane(step, slot, plane, rows_of):
+        total = 0
         for start in range(0, half, chunk):
-            at = pl.ds(PAD + start, chunk)
-            here = pl.ds(start, chunk)
-            pulled = pulls(step, slot, plane, bonds_of(pattern, plane, start), mask, start)
-            level = trial[slot, colour, plane - 1, 0, here]
-            draw = [trial[slot, colour, plane - 1, part, here] for part in (1, 2, 3)]
-            fresh = heated(pulled, beta, level, draw)
-            for part in range(3):
-                state[step + 1, slot, plane, part, at] = fresh[part]
-            gain = gain + jnp.sum(dot(fresh, pulled).reshape(-1, 8, columns), axis=0)
+            total = total + rows_of(step, slot, plane, start)
         wrap_rows(step + 1, slot, plane)
-        return gain
-
-    def halves(step, slot, body, initial, send=True, swap=False):
-        def visit(index, carry):
-            outer = index < 2
-            low = outer & (lax.rem(index + me, 2) == 0)
-            high = outer & (lax.rem(index + me, 2) == 1)
-            plane = jnp.where(low, 1, jnp.where(high, planes, index))
-
-            @pl.when(low)
-            def _():
-                upward(step, slot).wait_recv()
-
-            @pl.when(high)
-            def _():
-                downward(step, slot).wait_recv()
-
-            carry = body(step, slot, plane, carry)
+        return total
+
+    def outer_planes(step, slot, rows_of, send, swap):
+        total = 0
+        for part in range(CHUNKS):
+            far_in(step, slot, part).wait_recv()
+            for start in range(part * piece, (part + 1) * piece, chunk):
+                total = total + rows_of(step, slot, far_plane, start)
             if send:
-
-                @pl.when(low)
-                def _():
-                    downward(step + 1, slot).start()
-
-                @pl.when(high)
-                def _():
-                    upward(step + 1, slot).start()
-
+                far_out(step, slot, part).wait_send()
+                far_out(step + 1, slot, part).start()
+        wrap_rows(step + 1, slot, far_plane)
+        near_in(step, slot).wait_recv()
+        total = total + whole_plane(step, slot, near_plane, rows_of)
+        if send:
+            near_out(step, slot).wait_send()
+            near_out(step + 1, slot).start()
+        if swap:
+            swap_copy(slot, far_plane).start()
+            swap_copy(slot, near_plane).start()
+        return total
+
+    def inner_planes(step, slot, rows_of, swap, initial):
+        def visit(plane, total):
+            total = total + whole_plane(step, slot, plane, rows_of)
             if swap:
                 swap_copy(slot, plane).start()
-            return carry
-
-        return lax.fori_loop(0, planes, visit, initial)
-
-    def relax_body(step, slot, plane, carry):
-        relax_plane(step, slot, plane)
-        return carry
-
-    def heat_body(step, slot, plane, carry):
-        return carry + heat_plane(step, slot, plane)
-
-    share = planes // OR_HALVES
+            return total
+
+        return lax.fori_loop(2, planes, visit, initial)
+
+    zero = jnp.zeros((8, columns), jnp.float32)
+
+    def first_inner(slot, _):
+        inner_planes(1, slot, relax_rows, False, 0)
+        return 0
+
+    lax.fori_loop(0, 2, first_inner, 0)
+    for load in loads[1:]:
+        load.wait()
+
+    def fill(visit, _):
+        slot = visit // planes
+        plane = lax.rem(visit, planes)
+        pack_heat(slot, plane)
+        draw_copy(slot, plane).start()
+        return 0
+
+    lax.fori_loop(0, 2 * planes, fill, 0)
+    bond_up.wait_recv()
+    even, odd = bond_halo[even_rows, :], bond_halo[odd_rows, :]
+    bond_z[0, 0] = jnp.where(lane == 0, even, odd)
+    bond_z[1, 0] = jnp.where(lane == 0, odd, even)
 
     def relax_round(visit, _):
         step = visit // 2 + 1
         slot = lax.rem(visit, 2)
-        halves(step, slot, relax_body, 0)
-
-        def fill(index, _):
-            plane = (step - 1) * share + index
-            pack_heat(slot, plane)
-            draw_copy(slot, plane).start()
-            return 0
-
-        lax.fori_loop(0, share, fill, 0)
+        outer_planes(step, slot, relax_rows, True, False)
+        inner_planes(step + 1, slot, relax_rows, False, 0)
 
         @pl.when(visit == 1)
         def _():
@@ -484,14 +541,20 @@
 
         return 0
 
-    lax.fori_loop(0, 2 * OR_HALVES, relax_round, 0)
+    lax.fori_loop(0, 2 * (OR_HALVES - 1), relax_round, 0)
+
+    def last_relax(slot, _):
+        outer_planes(OR_HALVES, slot, relax_rows, True, False)
+        inner_planes(OR_HALVES + 1, slot, heat_rows, True, zero)
+        return 0
+
+    lax.fori_loop(0, 2, last_relax, 0)
     far_wait(0)
     far_signal(1)
 
-    zero = jnp.zeros((8, columns), jnp.float32)
-
     def first_heat(slot, _):
-        halves(OR_HALVES + 1, slot, heat_body, zero, swap=True)
+        outer_planes(OR_HALVES + 1, slot, heat_rows, True, True)
+        gains[slot] = inner_planes(OR_HALVES + 2, slot, heat_rows, False, zero)
         return 0
 
     lax.fori_loop(0, 2, first_heat, 0)
@@ -499,32 +562,46 @@
     far_signal(2)
 
     def second_heat(slot, _):
-        gain = halves(OR_HALVES + 2, slot, heat_body, zero, send=False)
+        gain = gains[slot] + outer_planes(OR_HALVES + 2, slot, heat_rows, False, False)
         share_sum[pl.ds(slot, 1), :] = jnp.sum(gain, axis=0, keepdims=True)
         return 0
 
     lax.fori_loop(0, 2, second_heat, 0)
     far_wait(2)
 
-    def give_share(distance, _):
-        share_copy(distance).start()
-        return 0
-
-    lax.fori_loop(1, count, give_share, 0)
-
-    def pass_on(slot, _):
-        swap_copy(1 - slot, 1).wait_recv()
-        downward(got, slot).start()
-        swap_copy(1 - slot, planes).wait_recv()
-        upward(got, slot).start()
-        return 0
-
-    lax.fori_loop(0, 2, pass_on, 0)
+    share_copy(count // 2).start()
+
+    def give_share(index, _):
+        share_copy(count // 2 - index).start()
+        share_copy(count // 2 + index).start()
+        return 0
+
+    lax.fori_loop(1, count // 2, give_share, 0)
+
+    def pass_far(slot, _):
+        swap_copy(1 - slot, far_plane).wait_recv()
+        for part in range(CHUNKS):
+            far_out(HALVES, slot, part).wait_send()
+            far_out(got, slot, part).start()
+        wrap_rows(got, slot, far_plane)
+        return 0
+
+    def pass_near(slot, _):
+        swap_copy(1 - slot, near_plane).wait_recv()
+        near_out(HALVES, slot).wait_send()
+        near_out(got, slot).start()
+        wrap_rows(got, slot, near_plane)
+        return 0
+
+    lax.fori_loop(0, 2, pass_far, 0)
+    lax.fori_loop(0, 2, pass_near, 0)
+    for slot in (0, 1):
+        all_draws(1 - slot).wait_recv()
+        meta_copy(1 - slot).wait_recv()
 
     def prepare(visit, _):
         slot = visit // planes
         plane = lax.rem(visit, planes)
-        draw_copy(1 - slot, plane).wait_recv()
         for start in range(0, half, chunk):
             here = pl.ds(start, chunk)
             level, height, angle = (draws_got[slot, plane, kind, here] for kind in range(3))
@@ -537,15 +614,6 @@
         return 0
 
     lax.fori_loop(0, 2 * planes, prepare, 0)
-
-    def take_share(distance, sums):
-        share_copy(distance).wait_recv()
-        return sums + share_got[distance - 1]
-
-    total_sum[...] = lax.fori_loop(1, count, take_share, share_sum[...])
-    for slot in (0, 1):
-        total_copy(slot).start()
-        meta_copy(1 - slot).wait_recv()
 
     taking = [
         (meta_got[0, 2:3] > 0.5) & (here_temp > 0),
@@ -582,24 +650,60 @@
                     unpack_mask, second, first
                 )
 
+    def arrive(visit, _):
+        slot = visit // (planes - 2)
+        plane = lax.rem(visit, planes - 2) + 2
+        swap_copy(1 - slot, plane).wait_recv()
+        wrap_rows(got, slot, plane)
+        return 0
+
+    lax.fori_loop(0, 2 * (planes - 2), arrive, 0)
+
+    def finish_inner(plane, _):
+        for slot in (0, 1):
+            finish_plane(slot, plane)
+        return 0
+
+    lax.fori_loop(2, planes, finish_inner, 0)
+
+    def finish_outer(index, _):
+        @pl.when(index == 0)
+        def _():
+            for slot in (0, 1):
+                near_in(got, slot).wait_recv()
+
+        @pl.when(index == 1)
+        def _():
+            for slot in (0, 1):
+                for part in range(CHUNKS):
+                    far_in(got, slot, part).wait_recv()
+
+        plane = jnp.where(index == 0, near_plane, far_plane)
+        for slot in (0, 1):
+            finish_plane(slot, plane)
+        return 0
+
+    lax.fori_loop(0, 2, finish_outer, 0)
+
+    all_shares.wait_recv()
+    total_sum[...] = share_sum[...] + jnp.sum(share_got[...], axis=0)
     for slot in (0, 1):
-
-        def arrive(plane, _, slot=slot):
-            @pl.when((plane > 1) & (plane < planes))
-            def _():
-                swap_copy(1 - slot, plane).wait_recv()
-
-            wrap_rows(got, slot, plane)
-            return 0
-
-        def inner(plane, _, slot=slot):
-            finish_plane(slot, plane)
-            return 0
-
-        lax.fori_loop(1, planes + 1, arrive, 0)
-        upward(got, slot).wait_recv()
-        downward(got, slot).wait_recv()
-        lax.fori_loop(1, planes + 1, inner, 0)
+        total_copy(slot).start()
+
+    bond_up.wait_send()
+    all_shares.wait_send()
+    for slot in (0, 1):
+        meta_copy(slot).wait_send()
+        all_draws(slot).wait_send()
+        for part in range(CHUNKS):
+            far_out(got, slot, part).wait_send()
+        near_out(got, slot).wait_send()
+
+    def drain_swap(index, _):
+        swap_copy(index // planes, lax.rem(index, planes) + 1).wait_send()
+        return 0
+
+    lax.fori_loop(0, 2 * planes, drain_swap, 0)
 
     for slot in (0, 1):
         total_copy(1 - slot).wait_recv()
@@ -609,37 +713,8 @@
         sites = float(columns * rows * planes * count)
         energy_ref[slot] = -jnp.sum(value) / sites
 
-    bond_up.wait_send()
     for slot in (0, 1):
-        meta_copy(slot).wait_send()
         total_copy(slot).wait_send()
-
-    def drain_halo(index, _):
-        step = index // 2 + 1
-        slot = lax.rem(index, 2)
-        upward(step, slot).wait_send()
-        downward(step, slot).wait_send()
-        return 0
-
-    lax.fori_loop(0, 2 * HALVES, drain_halo, 0)
-    for slot in (0, 1):
-        upward(got, slot).wait_send()
-        downward(got, slot).wait_send()
-
-    def drain_temp(index, _):
-        slot = index // planes
-        plane = lax.rem(index, planes)
-        draw_copy(slot, plane).wait_send()
-        swap_copy(slot, plane + 1).wait_send()
-        return 0
-
-    lax.fori_loop(0, 2 * planes, drain_temp, 0)
-
-    def drain_share(distance, _):
-        share_copy(distance).wait_send()
-        return 0
-
-    lax.fori_loop(1, count, drain_share, 0)
 
 
 def on_device(
@@ -664,12 +739,15 @@
     return pl.pallas_call(
         step_kernel,
         out_shape=(
-            jax.ShapeDtypeStruct(spin_state.shape, f32),
+            pltpu.VMEM(spin_state.shape, f32),
             jax.ShapeDtypeStruct((slots,), f32),
         ),
-        in_specs=[any_space] * 5 + [smem] * 3,
+        in_specs=[any_space] * 8,
         out_specs=(vmem, smem),
         scratch_shapes=[
+            pltpu.SMEM((slots,), f32),
+            pltpu.SMEM((slots,), jnp.int32),
+            pltpu.SMEM((slots,), jnp.int32),
             pltpu.VMEM(spin_state.shape, f32),
             pltpu.VMEM(couplings.shape, f32),
             pltpu.VMEM((3,) + heat_level.shape, f32),
@@ -689,19 +767,22 @@
             pltpu.VMEM((count - 1, 2, columns), f32),
             pltpu.VMEM((2, columns), f32),
             pltpu.VMEM((slots, 2, columns), f32),
-            dma((5,)),
+            pltpu.VMEM((slots, 8, columns), f32),
+            dma((3,)),
+            dma((planes,)),
+            dma((4,)),
             dma,
             dma,
-            dma((steps, slots, 2)),
-            dma((steps, slots, 2)),
+            dma((slots, CHUNKS + 1)),
+            dma((2, slots, CHUNKS + 1)),
             dma((slots,)),
+            dma((slots,)),
+            dma,
             dma((slots,)),
             dma((slots, planes)),
             dma((slots, planes)),
-            dma((slots, planes + 1)),
-            dma((slots, planes + 1)),
-            dma((count - 1,)),
-            dma((count - 1,)),
+            dma,
+            dma,
             dma((slots,)),
             dma((slots,)),
             pltpu.SemaphoreType.REGULAR((max(1, len(far_distances(count))),)),

time: 68.1 us -> 59.6 us (0.88)
  Pallas kernels: 64.1 us -> 57.2 us
  local copies, waits for them, and re-layouts: 3.22 us -> 1.66 us
    pallas_call x1, Pallas kernels: 64.1 us -> 57.2 us  [on_device(): pl.pallas_call(step_kernel, out_shape=(pltpu.VMEM(spin_state.shape, f32),...]
    unnamed x4, local copies, waits for them, and re-layouts: 3.22 us -> 1.66 us
where the time goes in v3:
time: 59.6 us; the launch traced here: 59.5 us
  Pallas kernels  57.2 us (96%)
  local copies, waits for them, and re-layouts  1.66 us (3%)
  between operations  0.65 us (1%)
    pallas_call x1, Pallas kernels, on_device(): pl.pallas_call(step_kernel, out_shape=(pltpu.VMEM(spin_state.shape, f32),...  57.2 us
    unnamed x4, local copies, waits for them, and re-layouts  1.66 us

profile of v3, /device:TPU:40, one launch (start us, length us, event | category | flops | bytes accessed | tf_op | source)
XLA Modules:
  0.0 59.5 jit_solution(9285965341893435362)
XLA Ops:
  0.6 57.2 %replica_step.1 = (f32[2,3,4,128,128]{4,3,2,1,0:T(8,128)S(1)}, f32[2]{0:T(128)}) custom-call(f32[2,3,4,128,128]{4,3,2,1,0:T(8,128)} %spin_hbm.1, f32[3,4,128,128]{3,2,1,0:T(8,128)} %bond_hbm.1, f32[2,4,128,128]{3,2,1,0:T(8,128)} %level_hbm.1, f32[2,4,128,128]{3,2,1,0:T(8,128)} %height_hbm.1, f32[2,4,128,128]{3,2,1,0:T(8,128)} %angle_hbm.1, f32[2]{0:T(128)} %beta_hbm.1, ...), custom_call_target="tpu_custom_call" | custom-call | tf_op jit(solution)/shard_map/replica_step/pallas_call | solution.py:739
  57.8 0.0 copy-start
  57.8 1.1 %copy.12 = f32[2,3,4,128,128]{4,3,2,1,0:T(8,128)} copy(f32[2,3,4,128,128]{4,3,2,1,0:T(8,128)S(1)} %get-tuple-element.2) | data formatting | bytes 3145728
  59.0 0.0 copy-done
  59.0 0.5 copy.13
Async XLA Ops:
  57.8 1.2 %copy-start = (f32[2]{0:T(128)S(1)}, f32[2]{0:T(128)}, u32[]{:S(2)}) copy-start(f32[2]{0:T(128)} %get-tuple-element.7) | copy-start | bytes 28

commit v4 on v3

--- a/solution.py
+++ b/solution.py
@@ -114,7 +114,7 @@
     planes, rows, columns = spin_in.shape[2:]
     half = rows // 2
     piece = half // CHUNKS
-    chunk = min(16, piece)
+    chunk = min(32, half)
     me = lax.axis_index("gz")
     count = lax.axis_size("gz")
     upper = lax.rem(me + 1, count)
@@ -170,6 +170,9 @@
 
     lane = lax.broadcasted_iota(jnp.int32, (half, columns), 1) % 2
     lane_chunk = lax.broadcasted_iota(jnp.int32, (chunk, columns), 1) % 2
+    def lane_piece(size):
+        return lax.broadcasted_iota(jnp.int32, (size, columns), 1) % 2
+
     for load in small:
         load.wait()
     swapped = bits_ref[0] != 0
@@ -195,7 +198,7 @@
             src_ref=state.at[step, slot, jnp.where(down, 1, planes), :, rows_at],
             dst_ref=state.at[step, slot, jnp.where(down, planes + 1, 0), :, rows_at],
             send_sem=send_sem.at[slot, part],
-            recv_sem=recv_sem.at[1 if step is got else lax.rem(step, 2), slot, part],
+            recv_sem=recv_sem.at[2 if isinstance(step, int) and step == got else lax.rem(step, 2), slot, part],
             device_id={"gz": jnp.where(down, lower, upper)},
             device_id_type=MESH,
         )
@@ -398,8 +401,8 @@
                 trial[slot, colour, plane, 2, here] = across * sine
                 trial[slot, colour, plane, 3, here] = height
 
-    def bonds_of(pattern, plane, start):
-        here = pl.ds(start, chunk)
+    def bonds_of(pattern, plane, start, size=chunk):
+        here = pl.ds(start, size)
         return (
             bond_x[pattern, plane - 1, 0, here],
             bond_x[pattern, plane - 1, 1, here],
@@ -409,16 +412,16 @@
             bond_z[pattern, plane - 1, here],
         )
 
-    def pulls(step, slot, plane, bonds, mask, start):
+    def pulls(step, slot, plane, bonds, mask, start, size=chunk):
         east, west, near, far, above, below = bonds
-        at = pl.ds(PAD + start, chunk)
+        at = pl.ds(PAD + start, size)
         out = []
         for part in range(3):
             centre = state[step, slot, plane, part, at]
             other = jnp.where(
                 mask,
-                state[step, slot, plane, part, pl.ds(PAD + start - 1, chunk)],
-                state[step, slot, plane, part, pl.ds(PAD + start + 1, chunk)],
+                state[step, slot, plane, part, pl.ds(PAD + start - 1, size)],
+                state[step, slot, plane, part, pl.ds(PAD + start + 1, size)],
             )
             pulled = east * pltpu.roll(centre, columns - 1, 1) + west * pltpu.roll(centre, 1, 1)
             pulled = pulled + near * centre + far * other
@@ -433,11 +436,11 @@
     def colour_of(step, slot, plane):
         return lax.rem(parity(slot, plane - 1) + step + 1, 2)
 
-    def relax_rows(step, slot, plane, start):
+    def relax_rows(step, slot, plane, start, size):
         pattern = colour_of(step, slot, plane)
-        at = pl.ds(PAD + start, chunk)
-        bonds = bonds_of(pattern, plane, start)
-        pulled = pulls(step, slot, plane, bonds, lane_chunk == pattern, start)
+        at = pl.ds(PAD + start, size)
+        bonds = bonds_of(pattern, plane, start, size)
+        pulled = pulls(step, slot, plane, bonds, lane_piece(size) == pattern, start, size)
         old = [state[step - 1, slot, plane, part, at] for part in range(3)]
         scale = 2.0 * dot(old, pulled) / jnp.maximum(dot(pulled, pulled), 0.01)
         for part in range(3):
@@ -456,13 +459,13 @@
         side = jnp.sqrt(jnp.maximum(1.0 - cosine * cosine, 0.0)) * norm
         return [cosine * axis[part] + side * tangent[part] for part in range(3)]
 
-    def heat_rows(step, slot, plane, start):
+    def heat_rows(step, slot, plane, start, size):
         colour = step - OR_HALVES - 1
         pattern = colour_of(step, slot, plane)
-        at = pl.ds(PAD + start, chunk)
-        here = pl.ds(start, chunk)
-        bonds = bonds_of(pattern, plane, start)
-        pulled = pulls(step, slot, plane, bonds, lane_chunk == pattern, start)
+        at = pl.ds(PAD + start, size)
+        here = pl.ds(start, size)
+        bonds = bonds_of(pattern, plane, start, size)
+        pulled = pulls(step, slot, plane, bonds, lane_piece(size) == pattern, start, size)
         level = trial[slot, colour, plane - 1, 0, here]
         draw = [trial[slot, colour, plane - 1, part, here] for part in (1, 2, 3)]
         fresh = heated(pulled, beta_of(slot), level, draw)
@@ -473,7 +476,7 @@
     def whole_plane(step, slot, plane, rows_of):
         total = 0
         for start in range(0, half, chunk):
-            total = total + rows_of(step, slot, plane, start)
+            total = total + rows_of(step, slot, plane, start, chunk)
         wrap_rows(step + 1, slot, plane)
         return total
 
@@ -481,8 +484,7 @@
         total = 0
         for part in range(CHUNKS):
             far_in(step, slot, part).wait_recv()
-            for start in range(part * piece, (part + 1) * piece, chunk):
-                total = total + rows_of(step, slot, far_plane, start)
+            total = total + rows_of(step, slot, far_plane, part * piece, piece)
             if send:
                 far_out(step, slot, part).wait_send()
                 far_out(step + 1, slot, part).start()
@@ -561,30 +563,28 @@
     far_wait(1)
     far_signal(2)
 
-    def second_heat(slot, _):
+    def second_heat(slot):
         gain = gains[slot] + outer_planes(OR_HALVES + 2, slot, heat_rows, False, False)
-        share_sum[pl.ds(slot, 1), :] = jnp.sum(gain, axis=0, keepdims=True)
-        return 0
-
-    lax.fori_loop(0, 2, second_heat, 0)
-    far_wait(2)
-
-    share_copy(count // 2).start()
-
-    def give_share(index, _):
-        share_copy(count // 2 - index).start()
-        share_copy(count // 2 + index).start()
-        return 0
-
-    lax.fori_loop(1, count // 2, give_share, 0)
-
-    def pass_far(slot, _):
+        share_sum[slot : slot + 1, :] = jnp.sum(gain, axis=0, keepdims=True)
+
+    def pass_far(slot):
         swap_copy(1 - slot, far_plane).wait_recv()
         for part in range(CHUNKS):
             far_out(HALVES, slot, part).wait_send()
             far_out(got, slot, part).start()
         wrap_rows(got, slot, far_plane)
-        return 0
+
+    second_heat(0)
+    second_heat(1)
+    far_wait(2)
+    share_copy(count // 2).start()
+
+    def give_share(index, _):
+        share_copy(count // 2 - index).start()
+        share_copy(count // 2 + index).start()
+        return 0
+
+    lax.fori_loop(1, count // 2, give_share, 0)
 
     def pass_near(slot, _):
         swap_copy(1 - slot, near_plane).wait_recv()
@@ -593,7 +593,8 @@
         wrap_rows(got, slot, near_plane)
         return 0
 
-    lax.fori_loop(0, 2, pass_far, 0)
+    pass_far(1)
+    pass_far(0)
     lax.fori_loop(0, 2, pass_near, 0)
     for slot in (0, 1):
         all_draws(1 - slot).wait_recv()
@@ -666,6 +667,11 @@
 
     lax.fori_loop(2, planes, finish_inner, 0)
 
+    all_shares.wait_recv()
+    total_sum[...] = share_sum[...] + jnp.sum(share_got[...], axis=0)
+    for slot in (0, 1):
+        total_copy(slot).start()
+
     def finish_outer(index, _):
         @pl.when(index == 0)
         def _():
@@ -684,11 +690,6 @@
         return 0
 
     lax.fori_loop(0, 2, finish_outer, 0)
-
-    all_shares.wait_recv()
-    total_sum[...] = share_sum[...] + jnp.sum(share_got[...], axis=0)
-    for slot in (0, 1):
-        total_copy(slot).start()
 
     bond_up.wait_send()
     all_shares.wait_send()
@@ -774,7 +775,7 @@
             dma,
             dma,
             dma((slots, CHUNKS + 1)),
-            dma((2, slots, CHUNKS + 1)),
+            dma((3, slots, CHUNKS + 1)),
             dma((slots,)),
             dma((slots,)),
             dma,

time: 59.6 us -> 58.6 us (0.983)
  Pallas kernels: 57.2 us -> 56 us
    pallas_call x1, Pallas kernels: 57.2 us -> 56 us  [on_device(): pl.pallas_call(step_kernel, out_shape=(pltpu.VMEM(spin_state.shape, f32),...]
where the time goes in v4:
time: 58.6 us; the launch traced here: 58.3 us
  Pallas kernels  56 us (96%)
  local copies, waits for them, and re-layouts  1.66 us (3%)
  between operations  0.65 us (1%)
    pallas_call x1, Pallas kernels, on_device(): pl.pallas_call(step_kernel, out_shape=(pltpu.VMEM(spin_state.shape, f32),...  56 us
    unnamed x4, local copies, waits for them, and re-layouts  1.66 us

profile of v4, /device:TPU:40, one launch (start us, length us, event | category | flops | bytes accessed | tf_op | source)
XLA Modules:
  0.0 58.3 jit_solution(931111029474147192)
XLA Ops:
  0.6 56.0 %replica_step.1 = (f32[2,3,4,128,128]{4,3,2,1,0:T(8,128)S(1)}, f32[2]{0:T(128)}) custom-call(f32[2,3,4,128,128]{4,3,2,1,0:T(8,128)} %spin_hbm.1, f32[3,4,128,128]{3,2,1,0:T(8,128)} %bond_hbm.1, f32[2,4,128,128]{3,2,1,0:T(8,128)} %level_hbm.1, f32[2,4,128,128]{3,2,1,0:T(8,128)} %height_hbm.1, f32[2,4,128,128]{3,2,1,0:T(8,128)} %angle_hbm.1, f32[2]{0:T(128)} %beta_hbm.1, ...), custom_call_target="tpu_custom_call" | custom-call | tf_op jit(solution)/shard_map/replica_step/pallas_call | solution.py:740
  56.6 0.0 copy-start
  56.6 1.1 %copy.12 = f32[2,3,4,128,128]{4,3,2,1,0:T(8,128)} copy(f32[2,3,4,128,128]{4,3,2,1,0:T(8,128)S(1)} %get-tuple-element.2) | data formatting | bytes 3145728
  57.8 0.0 copy-done
  57.8 0.5 copy.13
Async XLA Ops:
  56.6 1.2 %copy-start = (f32[2]{0:T(128)S(1)}, f32[2]{0:T(128)}, u32[]{:S(2)}) copy-start(f32[2]{0:T(128)} %get-tuple-element.7) | copy-start | bytes 28

commit v5 on v4

--- a/solution.py
+++ b/solution.py
@@ -81,6 +81,7 @@
     bond_ys,
     bond_z,
     bond_halo,
+    bond_top,
     trial,
     meta,
     meta_got,
@@ -149,6 +150,8 @@
     ]
     for load in small:
         load.start()
+    top_load = pltpu.make_async_copy(bond_hbm.at[2, planes - 1], bond_top, load_sem.at[4])
+    top_load.start()
     plane_order = [far_plane, near_plane] + list(range(2, planes))
     for plane in plane_order:
         spin_load(plane).start()
@@ -216,7 +219,7 @@
         return halo(step, slot, far_low, main, CHUNKS)
 
     bond_up = pltpu.make_async_remote_copy(
-        src_ref=bond_hbm.at[2, planes - 1],
+        src_ref=bond_top,
         dst_ref=bond_halo,
         send_sem=bond_send,
         recv_sem=bond_recv,
@@ -257,10 +260,18 @@
         return along_temp(
             state.at[HALVES, slot, plane, :, main],
             state.at[got, 1 - slot, plane, :, main],
-            swap_send.at[slot, plane - 1],
+            swap_send,
             swap_recv.at[1 - slot, plane - 1],
             slot,
         )
+
+    all_swaps = along_temp(
+        state.at[HALVES, :, pl.ds(1, planes), :, main],
+        state.at[got, :, pl.ds(1, planes), :, main],
+        swap_send,
+        swap_recv.at[0, 0],
+        0,
+    )
 
     def total_copy(slot):
         return along_temp(
@@ -330,18 +341,46 @@
         for slot in (0, 1):
             wrap_rows(1, slot, plane)
 
+    def first_copy(slot, down, rows_at, part):
+        return pltpu.make_async_remote_copy(
+            src_ref=state.at[jnp.where(down, 1, 0), slot, jnp.where(down, 1, 0), :, rows_at],
+            dst_ref=state.at[1, slot, jnp.where(down, planes + 1, 0), :, rows_at],
+            send_sem=send_sem.at[slot, part],
+            recv_sem=recv_sem.at[1, slot, part],
+            device_id={"gz": jnp.where(down, lower, upper)},
+            device_id_type=MESH,
+        )
+
+    def stage_products():
+        even, odd = bond_top[even_rows, :], bond_top[odd_rows, :]
+        for slot in (0, 1):
+            bond = jnp.where(lane == parity(slot, planes - 1), odd, even)
+            for part in range(3):
+                state[0, slot, 0, part, main] = bond * state[1, slot, planes, part, main]
+
     pl.semaphore_wait(barrier, 4)
-    bond_up.start()
+    top_load.wait()
     spin_load(far_plane).wait()
     pack_spins(far_plane)
+
+    @pl.when(~far_low)
+    def _():
+        stage_products()
+
     for slot in (0, 1):
         for part in range(CHUNKS):
-            far_out(1, slot, part).start()
+            first_copy(slot, far_low, pl.ds(PAD + part * piece, piece), part).start()
     spin_load(near_plane).wait()
     pack_spins(near_plane)
+
+    @pl.when(far_low)
+    def _():
+        stage_products()
+
     for slot in (0, 1):
-        near_out(1, slot).start()
+        first_copy(slot, ~far_low, main, CHUNKS).start()
         meta_copy(slot).start()
+    bond_up.start()
 
     def pack_inner(plane, _):
         spin_load(plane).wait()
@@ -480,7 +519,7 @@
         wrap_rows(step + 1, slot, plane)
         return total
 
-    def outer_planes(step, slot, rows_of, send, swap):
+    def far_rows(step, slot, rows_of, send, swap):
         total = 0
         for part in range(CHUNKS):
             far_in(step, slot, part).wait_recv()
@@ -489,15 +528,26 @@
                 far_out(step, slot, part).wait_send()
                 far_out(step + 1, slot, part).start()
         wrap_rows(step + 1, slot, far_plane)
+        if swap:
+            swap_copy(slot, far_plane).start()
+        return total
+
+    def near_rows(step, slot, rows_of, send, swap):
         near_in(step, slot).wait_recv()
-        total = total + whole_plane(step, slot, near_plane, rows_of)
+        total = whole_plane(step, slot, near_plane, rows_of)
         if send:
             near_out(step, slot).wait_send()
             near_out(step + 1, slot).start()
         if swap:
-            swap_copy(slot, far_plane).start()
             swap_copy(slot, near_plane).start()
         return total
+
+    def both(body):
+        def visit(slot, _):
+            body(slot)
+            return 0
+
+        lax.fori_loop(0, 2, visit, 0)
 
     def inner_planes(step, slot, rows_of, swap, initial):
         def visit(plane, total):
@@ -526,46 +576,50 @@
         return 0
 
     lax.fori_loop(0, 2 * planes, fill, 0)
-    bond_up.wait_recv()
-    even, odd = bond_halo[even_rows, :], bond_halo[odd_rows, :]
-    bond_z[0, 0] = jnp.where(lane == 0, even, odd)
-    bond_z[1, 0] = jnp.where(lane == 0, odd, even)
-
-    def relax_round(visit, _):
-        step = visit // 2 + 1
-        slot = lax.rem(visit, 2)
-        outer_planes(step, slot, relax_rows, True, False)
-        inner_planes(step + 1, slot, relax_rows, False, 0)
-
-        @pl.when(visit == 1)
+    bond_z[0, 0] = jnp.ones((half, columns), jnp.float32)
+    bond_z[1, 0] = jnp.ones((half, columns), jnp.float32)
+
+    def relax_round(step, _):
+        both(lambda slot: far_rows(step, slot, relax_rows, True, False))
+        both(lambda slot: near_rows(step, slot, relax_rows, True, False))
+
+        @pl.when(step == 1)
         def _():
             far_signal(0)
-
-        return 0
-
-    lax.fori_loop(0, 2 * (OR_HALVES - 1), relax_round, 0)
-
-    def last_relax(slot, _):
-        outer_planes(OR_HALVES, slot, relax_rows, True, False)
-        inner_planes(OR_HALVES + 1, slot, heat_rows, True, zero)
-        return 0
-
-    lax.fori_loop(0, 2, last_relax, 0)
+            bond_up.wait_recv()
+            even, odd = bond_halo[even_rows, :], bond_halo[odd_rows, :]
+            bond_z[0, 0] = jnp.where(lane == 0, even, odd)
+            bond_z[1, 0] = jnp.where(lane == 0, odd, even)
+
+        both(lambda slot: inner_planes(step + 1, slot, relax_rows, False, 0))
+        return 0
+
+    lax.fori_loop(1, OR_HALVES, relax_round, 0)
+    both(lambda slot: far_rows(OR_HALVES, slot, relax_rows, True, False))
+    both(lambda slot: near_rows(OR_HALVES, slot, relax_rows, True, False))
+    both(lambda slot: inner_planes(OR_HALVES + 1, slot, heat_rows, True, zero))
     far_wait(0)
     far_signal(1)
 
-    def first_heat(slot, _):
-        outer_planes(OR_HALVES + 1, slot, heat_rows, True, True)
+    both(lambda slot: far_rows(OR_HALVES + 1, slot, heat_rows, True, True))
+    both(lambda slot: near_rows(OR_HALVES + 1, slot, heat_rows, True, True))
+
+    def inner_gain(slot):
         gains[slot] = inner_planes(OR_HALVES + 2, slot, heat_rows, False, zero)
-        return 0
-
-    lax.fori_loop(0, 2, first_heat, 0)
+
+    def far_gain(slot):
+        gains[slot] = gains[slot] + far_rows(OR_HALVES + 2, slot, heat_rows, False, False)
+
+    def near_gain(slot):
+        gain = gains[slot] + near_rows(OR_HALVES + 2, slot, heat_rows, False, False)
+        share_sum[pl.ds(slot, 1), :] = jnp.sum(gain, axis=0, keepdims=True)
+
+    both(inner_gain)
     far_wait(1)
     far_signal(2)
-
-    def second_heat(slot):
-        gain = gains[slot] + outer_planes(OR_HALVES + 2, slot, heat_rows, False, False)
-        share_sum[slot : slot + 1, :] = jnp.sum(gain, axis=0, keepdims=True)
+    both(far_gain)
+    both(near_gain)
+    far_wait(2)
 
     def pass_far(slot):
         swap_copy(1 - slot, far_plane).wait_recv()
@@ -574,9 +628,6 @@
             far_out(got, slot, part).start()
         wrap_rows(got, slot, far_plane)
 
-    second_heat(0)
-    second_heat(1)
-    far_wait(2)
     share_copy(count // 2).start()
 
     def give_share(index, _):
@@ -584,7 +635,7 @@
         share_copy(count // 2 + index).start()
         return 0
 
-    lax.fori_loop(1, count // 2, give_share, 0)
+    lax.fori_loop(1, count // 2, give_share, 0, unroll=True)
 
     def pass_near(slot, _):
         swap_copy(1 - slot, near_plane).wait_recv()
@@ -700,19 +751,18 @@
             far_out(got, slot, part).wait_send()
         near_out(got, slot).wait_send()
 
-    def drain_swap(index, _):
-        swap_copy(index // planes, lax.rem(index, planes) + 1).wait_send()
-        return 0
-
-    lax.fori_loop(0, 2 * planes, drain_swap, 0)
+    all_swaps.wait_send()
 
     for slot in (0, 1):
         total_copy(1 - slot).wait_recv()
-        own = total_sum[slot : slot + 1]
-        other = total_got[slot, 1 - slot : 2 - slot]
-        value = jnp.where(taking[slot], other, own)
-        sites = float(columns * rows * planes * count)
-        energy_ref[slot] = -jnp.sum(value) / sites
+    sites = float(columns * rows * planes * count)
+    values = [
+        jnp.where(taking[slot], total_got[slot, 1 - slot : 2 - slot], total_sum[slot : slot + 1])
+        for slot in (0, 1)
+    ]
+    sums = [-jnp.sum(value, axis=1, keepdims=True) / sites for value in values]
+    spot = lax.broadcasted_iota(jnp.int32, (1, columns), 1)
+    energy_ref[...] = jnp.where(spot == 0, sums[0], sums[1])
 
     for slot in (0, 1):
         total_copy(slot).wait_send()
@@ -734,17 +784,16 @@
     f32 = jnp.float32
     dma = pltpu.SemaphoreType.DMA
     any_space = pl.BlockSpec(memory_space=pl.ANY)
-    smem = pl.BlockSpec(memory_space=pltpu.SMEM)
     vmem = pl.BlockSpec(memory_space=pltpu.VMEM)
     steps = HALVES + 3
-    return pl.pallas_call(
+    spins, energies = pl.pallas_call(
         step_kernel,
         out_shape=(
             pltpu.VMEM(spin_state.shape, f32),
-            jax.ShapeDtypeStruct((slots,), f32),
+            pltpu.VMEM((1, columns), f32),
         ),
         in_specs=[any_space] * 8,
-        out_specs=(vmem, smem),
+        out_specs=(vmem, vmem),
         scratch_shapes=[
             pltpu.SMEM((slots,), f32),
             pltpu.SMEM((slots,), jnp.int32),
@@ -757,6 +806,7 @@
             pltpu.VMEM((2, planes, half, columns), f32),
             pltpu.VMEM((planes, half, columns), f32),
             pltpu.VMEM((2, planes + 1, half, columns), f32),
+            pltpu.VMEM((rows, columns), f32),
             pltpu.VMEM((rows, columns), f32),
             pltpu.VMEM((slots, 2, planes, 4, half, columns), f32),
             pltpu.VMEM((slots, 8, columns), f32),
@@ -771,7 +821,7 @@
             pltpu.VMEM((slots, 8, columns), f32),
             dma((3,)),
             dma((planes,)),
-            dma((4,)),
+            dma((5,)),
             dma,
             dma,
             dma((slots, CHUNKS + 1)),
@@ -780,7 +830,7 @@
             dma((slots,)),
             dma,
             dma((slots,)),
-            dma((slots, planes)),
+            dma,
             dma((slots, planes)),
             dma,
             dma,
@@ -802,6 +852,7 @@
         colour_order,
         swap_bits,
     )
+    return (spins, energies[0, :slots])
 
 
 def solution(mesh):

time: 58.6 us -> 57.9 us (0.988)
    unnamed x4 -> x1, local copies, waits for them, and re-layouts: 1.66 us -> 1.15 us
where the time goes in v5:
time: 57.9 us; the launch traced here: 57.8 us
  Pallas kernels  55.5 us (96%)
  local copies, waits for them, and re-layouts  1.66 us (3%)
  between operations  0.64 us (1%)
    pallas_call x1, Pallas kernels, on_device(): pl.pallas_call(step_kernel, out_shape=(pltpu.VMEM(spin_state.shape, f32),...  55.5 us

profile of v5, /device:TPU:40, one launch (start us, length us, event | category | flops | bytes accessed | tf_op | source)
XLA Modules:
  0.0 57.8 jit_solution(17145772494338294332)
XLA Ops:
  0.6 55.5 %replica_step.1 = (f32[2,3,4,128,128]{4,3,2,1,0:T(8,128)S(1)}, f32[1,128]{1,0:T(1,128)S(1)}) custom-call(f32[2,3,4,128,128]{4,3,2,1,0:T(8,128)} %spin_hbm.1, f32[3,4,128,128]{3,2,1,0:T(8,128)} %bond_hbm.1, f32[2,4,128,128]{3,2,1,0:T(8,128)} %level_hbm.1, f32[2,4,128,128]{3,2,1,0:T(8,128)} %height_hbm.1, f32[2,4,128,128]{3,2,1,0:T(8,128)} %angle_hbm.1, ...), custom_call_target="tpu_custom_call" | custom-call | tf_op jit(solution)/shard_map/replica_step/pallas_call | solution.py:789
  56.1 1.1 %copy.11 = f32[2,3,4,128,128]{4,3,2,1,0:T(8,128)} copy(f32[2,3,4,128,128]{4,3,2,1,0:T(8,128)S(1)} %get-tuple-element.6) | data formatting | bytes 3145728
  57.2 0.5 slice_bitcast_fusion

commit v6 on v5

--- a/solution.py
+++ b/solution.py
@@ -126,6 +126,25 @@
     got = HALVES + 2
     distances = far_distances(count)
 
+    def temp_towards(slot):
+        return lax.rem(here_temp + 2 * slot - 1 + temps, temps)
+
+    def has(slot):
+        return (here_temp + slot > 0) & (here_temp + slot < temps)
+
+    barrier = pltpu.get_barrier_semaphore()
+    for neighbour in (lower, upper):
+        pl.semaphore_signal(
+            barrier, inc=1, device_id={"gz": neighbour}, device_id_type=MESH
+        )
+    for slot in (0, 1):
+
+        @pl.when(has(slot))
+        def _(slot=slot):
+            pl.semaphore_signal(
+                barrier, inc=1, device_id={"temp": temp_towards(slot)}, device_id_type=MESH
+            )
+
     far_low = lax.rem(me, 2) == 0
     far_plane = jnp.where(far_low, 1, planes)
     near_plane = jnp.where(far_low, planes, 1)
@@ -158,19 +177,6 @@
     for load in loads:
         load.start()
 
-    def temp_towards(slot):
-        return lax.rem(here_temp + 2 * slot - 1 + temps, temps)
-
-    barrier = pltpu.get_barrier_semaphore()
-    for neighbour in (lower, upper):
-        pl.semaphore_signal(
-            barrier, inc=1, device_id={"gz": neighbour}, device_id_type=MESH
-        )
-    for slot in (0, 1):
-        pl.semaphore_signal(
-            barrier, inc=1, device_id={"temp": temp_towards(slot)}, device_id_type=MESH
-        )
-
     lane = lax.broadcasted_iota(jnp.int32, (half, columns), 1) % 2
     lane_chunk = lax.broadcasted_iota(jnp.int32, (chunk, columns), 1) % 2
     def lane_piece(size):
@@ -246,32 +252,33 @@
         return along_temp(
             draws.at[slot, plane],
             draws_got.at[1 - slot, plane],
-            draw_send,
+            draw_send.at[slot],
             draw_recv.at[1 - slot],
             slot,
         )
 
     def all_draws(slot):
         return along_temp(
-            draws.at[slot], draws_got.at[1 - slot], draw_send, draw_recv.at[1 - slot], slot
+            draws.at[slot], draws_got.at[1 - slot], draw_send.at[slot], draw_recv.at[1 - slot], slot
         )
 
     def swap_copy(slot, plane):
         return along_temp(
             state.at[HALVES, slot, plane, :, main],
             state.at[got, 1 - slot, plane, :, main],
-            swap_send,
+            swap_send.at[slot],
             swap_recv.at[1 - slot, plane - 1],
             slot,
         )
 
-    all_swaps = along_temp(
-        state.at[HALVES, :, pl.ds(1, planes), :, main],
-        state.at[got, :, pl.ds(1, planes), :, main],
-        swap_send,
-        swap_recv.at[0, 0],
-        0,
-    )
+    def all_swaps(slot):
+        return along_temp(
+            state.at[HALVES, slot, pl.ds(1, planes), :, main],
+            state.at[got, 1 - slot, pl.ds(1, planes), :, main],
+            swap_send.at[slot],
+            swap_recv.at[0, 0],
+            slot,
+        )
 
     def total_copy(slot):
         return along_temp(
@@ -358,7 +365,7 @@
             for part in range(3):
                 state[0, slot, 0, part, main] = bond * state[1, slot, planes, part, main]
 
-    pl.semaphore_wait(barrier, 4)
+    pl.semaphore_wait(barrier, 2 + has(0).astype(jnp.int32) + has(1).astype(jnp.int32))
     top_load.wait()
     spin_load(far_plane).wait()
     pack_spins(far_plane)
@@ -379,7 +386,15 @@
 
     for slot in (0, 1):
         first_copy(slot, ~far_low, main, CHUNKS).start()
-        meta_copy(slot).start()
+
+        @pl.when(has(slot))
+        def _(slot=slot):
+            meta_copy(slot).start()
+
+        @pl.when(~has(slot))
+        def _(slot=slot):
+            meta_got[slot] = jnp.zeros((8, columns), jnp.float32)
+
     bond_up.start()
 
     def pack_inner(plane, _):
@@ -519,6 +534,11 @@
         wrap_rows(step + 1, slot, plane)
         return total
 
+    def swap_start(slot, plane):
+        @pl.when(has(slot))
+        def _():
+            swap_copy(slot, plane).start()
+
     def far_rows(step, slot, rows_of, send, swap):
         total = 0
         for part in range(CHUNKS):
@@ -529,7 +549,7 @@
                 far_out(step + 1, slot, part).start()
         wrap_rows(step + 1, slot, far_plane)
         if swap:
-            swap_copy(slot, far_plane).start()
+            swap_start(slot, far_plane)
         return total
 
     def near_rows(step, slot, rows_of, send, swap):
@@ -539,7 +559,7 @@
             near_out(step, slot).wait_send()
             near_out(step + 1, slot).start()
         if swap:
-            swap_copy(slot, near_plane).start()
+            swap_start(slot, near_plane)
         return total
 
     def both(body):
@@ -553,7 +573,7 @@
         def visit(plane, total):
             total = total + whole_plane(step, slot, plane, rows_of)
             if swap:
-                swap_copy(slot, plane).start()
+                swap_start(slot, plane)
             return total
 
         return lax.fori_loop(2, planes, visit, initial)
@@ -572,7 +592,11 @@
         slot = visit // planes
         plane = lax.rem(visit, planes)
         pack_heat(slot, plane)
-        draw_copy(slot, plane).start()
+
+        @pl.when(has(slot))
+        def _():
+            draw_copy(slot, plane).start()
+
         return 0
 
     lax.fori_loop(0, 2 * planes, fill, 0)
@@ -591,15 +615,20 @@
             bond_z[0, 0] = jnp.where(lane == 0, even, odd)
             bond_z[1, 0] = jnp.where(lane == 0, odd, even)
 
+        @pl.when(step == 2)
+        def _():
+            far_wait(0)
+            far_signal(1)
+
         both(lambda slot: inner_planes(step + 1, slot, relax_rows, False, 0))
         return 0
 
     lax.fori_loop(1, OR_HALVES, relax_round, 0)
     both(lambda slot: far_rows(OR_HALVES, slot, relax_rows, True, False))
     both(lambda slot: near_rows(OR_HALVES, slot, relax_rows, True, False))
+    far_wait(1)
+    far_signal(2)
     both(lambda slot: inner_planes(OR_HALVES + 1, slot, heat_rows, True, zero))
-    far_wait(0)
-    far_signal(1)
 
     both(lambda slot: far_rows(OR_HALVES + 1, slot, heat_rows, True, True))
     both(lambda slot: near_rows(OR_HALVES + 1, slot, heat_rows, True, True))
@@ -615,18 +644,20 @@
         share_sum[pl.ds(slot, 1), :] = jnp.sum(gain, axis=0, keepdims=True)
 
     both(inner_gain)
-    far_wait(1)
-    far_signal(2)
     both(far_gain)
     both(near_gain)
     far_wait(2)
 
     def pass_far(slot):
-        swap_copy(1 - slot, far_plane).wait_recv()
         for part in range(CHUNKS):
             far_out(HALVES, slot, part).wait_send()
-            far_out(got, slot, part).start()
-        wrap_rows(got, slot, far_plane)
+
+        @pl.when(has(slot))
+        def _():
+            swap_copy(1 - slot, far_plane).wait_recv()
+            for part in range(CHUNKS):
+                far_out(got, slot, part).start()
+            wrap_rows(got, slot, far_plane)
 
     share_copy(count // 2).start()
 
@@ -638,18 +669,25 @@
     lax.fori_loop(1, count // 2, give_share, 0, unroll=True)
 
     def pass_near(slot, _):
-        swap_copy(1 - slot, near_plane).wait_recv()
         near_out(HALVES, slot).wait_send()
-        near_out(got, slot).start()
-        wrap_rows(got, slot, near_plane)
+
+        @pl.when(has(slot))
+        def _():
+            swap_copy(1 - slot, near_plane).wait_recv()
+            near_out(got, slot).start()
+            wrap_rows(got, slot, near_plane)
+
         return 0
 
     pass_far(1)
     pass_far(0)
     lax.fori_loop(0, 2, pass_near, 0)
     for slot in (0, 1):
-        all_draws(1 - slot).wait_recv()
-        meta_copy(1 - slot).wait_recv()
+
+        @pl.when(has(slot))
+        def _(slot=slot):
+            all_draws(1 - slot).wait_recv()
+            meta_copy(1 - slot).wait_recv()
 
     def prepare(visit, _):
         slot = visit // planes
@@ -705,8 +743,12 @@
     def arrive(visit, _):
         slot = visit // (planes - 2)
         plane = lax.rem(visit, planes - 2) + 2
-        swap_copy(1 - slot, plane).wait_recv()
-        wrap_rows(got, slot, plane)
+
+        @pl.when(has(slot))
+        def _():
+            swap_copy(1 - slot, plane).wait_recv()
+            wrap_rows(got, slot, plane)
+
         return 0
 
     lax.fori_loop(0, 2 * (planes - 2), arrive, 0)
@@ -721,17 +763,20 @@
     all_shares.wait_recv()
     total_sum[...] = share_sum[...] + jnp.sum(share_got[...], axis=0)
     for slot in (0, 1):
-        total_copy(slot).start()
+
+        @pl.when(has(slot))
+        def _(slot=slot):
+            total_copy(slot).start()
 
     def finish_outer(index, _):
-        @pl.when(index == 0)
-        def _():
-            for slot in (0, 1):
+        for slot in (0, 1):
+
+            @pl.when((index == 0) & has(slot))
+            def _(slot=slot):
                 near_in(got, slot).wait_recv()
 
-        @pl.when(index == 1)
-        def _():
-            for slot in (0, 1):
+            @pl.when((index == 1) & has(slot))
+            def _(slot=slot):
                 for part in range(CHUNKS):
                     far_in(got, slot, part).wait_recv()
 
@@ -745,16 +790,22 @@
     bond_up.wait_send()
     all_shares.wait_send()
     for slot in (0, 1):
-        meta_copy(slot).wait_send()
-        all_draws(slot).wait_send()
-        for part in range(CHUNKS):
-            far_out(got, slot, part).wait_send()
-        near_out(got, slot).wait_send()
-
-    all_swaps.wait_send()
+
+        @pl.when(has(slot))
+        def _(slot=slot):
+            meta_copy(slot).wait_send()
+            all_draws(slot).wait_send()
+            all_swaps(slot).wait_send()
+            for part in range(CHUNKS):
+                far_out(got, slot, part).wait_send()
+            near_out(got, slot).wait_send()
 
     for slot in (0, 1):
-        total_copy(1 - slot).wait_recv()
+
+        @pl.when(has(slot))
+        def _(slot=slot):
+            total_copy(1 - slot).wait_recv()
+
     sites = float(columns * rows * planes * count)
     values = [
         jnp.where(taking[slot], total_got[slot, 1 - slot : 2 - slot], total_sum[slot : slot + 1])
@@ -765,7 +816,10 @@
     energy_ref[...] = jnp.where(spot == 0, sums[0], sums[1])
 
     for slot in (0, 1):
-        total_copy(slot).wait_send()
+
+        @pl.when(has(slot))
+        def _(slot=slot):
+            total_copy(slot).wait_send()
 
 
 def on_device(
@@ -828,9 +882,9 @@
             dma((3, slots, CHUNKS + 1)),
             dma((slots,)),
             dma((slots,)),
-            dma,
             dma((slots,)),
-            dma,
+            dma((slots,)),
+            dma((slots,)),
             dma((slots, planes)),
             dma,
             dma,

time: 57.9 us -> 54.3 us (0.938)
  Pallas kernels: 55.5 us -> 51.8 us
    pallas_call x1, Pallas kernels: 55.5 us -> 51.8 us  [on_device(): pl.pallas_call(step_kernel, out_shape=(pltpu.VMEM(spin_state.shape, f32),...]
where the time goes in v6:
time: 54.3 us; the launch traced here: 54.1 us
  Pallas kernels  51.8 us (95%)
  local copies, waits for them, and re-layouts  1.66 us (3%)
  between operations  0.64 us (1%)
    pallas_call x1, Pallas kernels, on_device(): pl.pallas_call(step_kernel, out_shape=(pltpu.VMEM(spin_state.shape, f32),...  51.8 us
    unnamed x1, local copies, waits for them, and re-layouts  1.15 us

profile of v6, /device:TPU:40, one launch (start us, length us, event | category | flops | bytes accessed | tf_op | source)
XLA Modules:
  0.0 54.1 jit_solution(5972618003834985296)
XLA Ops:
  0.6 51.8 %replica_step.1 = (f32[2,3,4,128,128]{4,3,2,1,0:T(8,128)S(1)}, f32[1,128]{1,0:T(1,128)S(1)}) custom-call(f32[2,3,4,128,128]{4,3,2,1,0:T(8,128)} %spin_hbm.1, f32[3,4,128,128]{3,2,1,0:T(8,128)} %bond_hbm.1, f32[2,4,128,128]{3,2,1,0:T(8,128)} %level_hbm.1, f32[2,4,128,128]{3,2,1,0:T(8,128)} %height_hbm.1, f32[2,4,128,128]{3,2,1,0:T(8,128)} %angle_hbm.1, ...), custom_call_target="tpu_custom_call" | custom-call | tf_op jit(solution)/shard_map/replica_step/pallas_call | solution.py:843
  52.4 1.1 %copy.11 = f32[2,3,4,128,128]{4,3,2,1,0:T(8,128)} copy(f32[2,3,4,128,128]{4,3,2,1,0:T(8,128)S(1)} %get-tuple-element.6) | data formatting | bytes 3145728
  53.6 0.5 slice_bitcast_fusion

commit v7 on v6

--- a/solution.py
+++ b/solution.py
@@ -207,7 +207,7 @@
             src_ref=state.at[step, slot, jnp.where(down, 1, planes), :, rows_at],
             dst_ref=state.at[step, slot, jnp.where(down, planes + 1, 0), :, rows_at],
             send_sem=send_sem.at[slot, part],
-            recv_sem=recv_sem.at[2 if isinstance(step, int) and step == got else lax.rem(step, 2), slot, part],
+            recv_sem=recv_sem.at[1 if isinstance(step, int) and step == got else lax.rem(step, 2), slot, part],
             device_id={"gz": jnp.where(down, lower, upper)},
             device_id_type=MESH,
         )
@@ -573,7 +573,11 @@
         def visit(plane, total):
             total = total + whole_plane(step, slot, plane, rows_of)
             if swap:
-                swap_start(slot, plane)
+
+                @pl.when(plane == 2)
+                def _():
+                    swap_start(slot, plane)
+
             return total
 
         return lax.fori_loop(2, planes, visit, initial)
@@ -630,8 +634,15 @@
     far_signal(2)
     both(lambda slot: inner_planes(OR_HALVES + 1, slot, heat_rows, True, zero))
 
-    both(lambda slot: far_rows(OR_HALVES + 1, slot, heat_rows, True, True))
+    both(lambda slot: far_rows(OR_HALVES + 1, slot, heat_rows, True, False))
+    both(lambda slot: swap_start(slot, far_plane))
     both(lambda slot: near_rows(OR_HALVES + 1, slot, heat_rows, True, True))
+
+    def rest_of_swap(visit, _):
+        swap_start(lax.rem(visit, 2), visit // 2 + 3)
+        return 0
+
+    lax.fori_loop(0, 2 * (planes - 3), rest_of_swap, 0)
 
     def inner_gain(slot):
         gains[slot] = inner_planes(OR_HALVES + 2, slot, heat_rows, False, zero)
@@ -659,14 +670,13 @@
                 far_out(got, slot, part).start()
             wrap_rows(got, slot, far_plane)
 
-    share_copy(count // 2).start()
-
-    def give_share(index, _):
-        share_copy(count // 2 - index).start()
-        share_copy(count // 2 + index).start()
-        return 0
-
-    lax.fori_loop(1, count // 2, give_share, 0, unroll=True)
+    close = min(3, count // 2 - 1)
+    sides = [side for step in range(1, close + 1) for side in (step, count - step)]
+    sides.append(count // 2)
+    for step in range(count // 2 - 1, close, -1):
+        sides += [step, count - step]
+    for distance in sides:
+        share_copy(distance).start()
 
     def pass_near(slot, _):
         near_out(HALVES, slot).wait_send()
@@ -740,6 +750,14 @@
                     unpack_mask, second, first
                 )
 
+    all_shares.wait_recv()
+    total_sum[...] = share_sum[...] + jnp.sum(share_got[...], axis=0)
+    for slot in (0, 1):
+
+        @pl.when(has(slot))
+        def _(slot=slot):
+            total_copy(slot).start()
+
     def arrive(visit, _):
         slot = visit // (planes - 2)
         plane = lax.rem(visit, planes - 2) + 2
@@ -759,14 +777,6 @@
         return 0
 
     lax.fori_loop(2, planes, finish_inner, 0)
-
-    all_shares.wait_recv()
-    total_sum[...] = share_sum[...] + jnp.sum(share_got[...], axis=0)
-    for slot in (0, 1):
-
-        @pl.when(has(slot))
-        def _(slot=slot):
-            total_copy(slot).start()
 
     def finish_outer(index, _):
         for slot in (0, 1):
@@ -879,7 +889,7 @@
             dma,
             dma,
             dma((slots, CHUNKS + 1)),
-            dma((3, slots, CHUNKS + 1)),
+            dma((2, slots, CHUNKS + 1)),
             dma((slots,)),
             dma((slots,)),
             dma((slots,)),

time: 54.3 us -> 53.6 us (0.987)
  Pallas kernels: 51.8 us -> 51.1 us
    pallas_call x1, Pallas kernels: 51.8 us -> 51.1 us  [on_device(): pl.pallas_call(step_kernel, out_shape=(pltpu.VMEM(spin_state.shape, f32),...]
where the time goes in v7:
time: 53.6 us; the launch traced here: 53.4 us
  Pallas kernels  51.1 us (95%)
  local copies, waits for them, and re-layouts  1.66 us (3%)
  between operations  0.64 us (1%)
    pallas_call x1, Pallas kernels, on_device(): pl.pallas_call(step_kernel, out_shape=(pltpu.VMEM(spin_state.shape, f32),...  51.1 us
    unnamed x1, local copies, waits for them, and re-layouts  1.15 us

profile of v7, /device:TPU:40, one launch (start us, length us, event | category | flops | bytes accessed | tf_op | source)
XLA Modules:
  0.0 53.4 jit_solution(3642498035143725623)
XLA Ops:
  0.6 51.1 %replica_step.1 = (f32[2,3,4,128,128]{4,3,2,1,0:T(8,128)S(1)}, f32[1,128]{1,0:T(1,128)S(1)}) custom-call(f32[2,3,4,128,128]{4,3,2,1,0:T(8,128)} %spin_hbm.1, f32[3,4,128,128]{3,2,1,0:T(8,128)} %bond_hbm.1, f32[2,4,128,128]{3,2,1,0:T(8,128)} %level_hbm.1, f32[2,4,128,128]{3,2,1,0:T(8,128)} %height_hbm.1, f32[2,4,128,128]{3,2,1,0:T(8,128)} %angle_hbm.1, ...), custom_call_target="tpu_custom_call" | custom-call | tf_op jit(solution)/shard_map/replica_step/pallas_call | solution.py:853
  51.7 1.1 %copy.11 = f32[2,3,4,128,128]{4,3,2,1,0:T(8,128)} copy(f32[2,3,4,128,128]{4,3,2,1,0:T(8,128)S(1)} %get-tuple-element.6) | data formatting | bytes 3145728
  52.8 0.5 slice_bitcast_fusion

commit v8 on v7

--- a/solution.py
+++ b/solution.py
@@ -635,8 +635,9 @@
     both(lambda slot: inner_planes(OR_HALVES + 1, slot, heat_rows, True, zero))
 
     both(lambda slot: far_rows(OR_HALVES + 1, slot, heat_rows, True, False))
+    both(lambda slot: near_rows(OR_HALVES + 1, slot, heat_rows, True, False))
     both(lambda slot: swap_start(slot, far_plane))
-    both(lambda slot: near_rows(OR_HALVES + 1, slot, heat_rows, True, True))
+    both(lambda slot: swap_start(slot, near_plane))
 
     def rest_of_swap(visit, _):
         swap_start(lax.rem(visit, 2), visit // 2 + 3)

time: 53.6 us -> 53.6 us (level)
  no operation moved by 1% of the time
where the time goes in v8:
time: 53.6 us; the launch traced here: 53.4 us
  Pallas kernels  51.1 us (95%)
  local copies, waits for them, and re-layouts  1.66 us (3%)
  between operations  0.64 us (1%)
    pallas_call x1, Pallas kernels, on_device(): pl.pallas_call(step_kernel, out_shape=(pltpu.VMEM(spin_state.shape, f32),...  51.1 us
    unnamed x1, local copies, waits for them, and re-layouts  1.15 us

profile of v8, /device:TPU:40, one launch (start us, length us, event | category | flops | bytes accessed | tf_op | source)
XLA Modules:
  0.0 53.4 jit_solution(15517501724468670336)
XLA Ops:
  0.6 51.1 %replica_step.1 = (f32[2,3,4,128,128]{4,3,2,1,0:T(8,128)S(1)}, f32[1,128]{1,0:T(1,128)S(1)}) custom-call(f32[2,3,4,128,128]{4,3,2,1,0:T(8,128)} %spin_hbm.1, f32[3,4,128,128]{3,2,1,0:T(8,128)} %bond_hbm.1, f32[2,4,128,128]{3,2,1,0:T(8,128)} %level_hbm.1, f32[2,4,128,128]{3,2,1,0:T(8,128)} %height_hbm.1, f32[2,4,128,128]{3,2,1,0:T(8,128)} %angle_hbm.1, ...), custom_call_target="tpu_custom_call" | custom-call | tf_op jit(solution)/shard_map/replica_step/pallas_call | solution.py:854
  51.7 1.1 %copy.11 = f32[2,3,4,128,128]{4,3,2,1,0:T(8,128)} copy(f32[2,3,4,128,128]{4,3,2,1,0:T(8,128)S(1)} %get-tuple-element.6) | data formatting | bytes 3145728
  52.8 0.5 slice_bitcast_fusion
